TPU v7x, 32 devices: a whole 2x2x4 slice. The times are simulated.
32 devices in a mesh: gx: 2 (over x), gy: 4 (over z), gz: 4 (over y, core).
Axes of the slice: x: 2, y: 2, z: 4, core: 2. Of those that a mesh axis runs over, the one named last changes fastest.
Arguments:
- vectors: float32 [3, 12, 24, 24, 128], P(None, 'gx', 'gy', 'gz'), may hold values from -6 to 6
- orient_flip: int32 [4, 8, 1152], P('gx', 'gy', 'gz'), may hold values from 0 to 1
- reluctivity: float32 [4, 8, 512], P('gx', 'gy', 'gz'), may hold values from 0.05 to 0.5
- conductivity: float32 [4, 8, 512], P('gx', 'gy', 'gz'), may hold values from 1 to 10
Outputs:
- out_x: float32 [12, 28, 28, 128], P('gx', 'gy', 'gz')
- out_y: float32 [14, 24, 28, 128], P('gx', 'gy', 'gz')
- out_z: float32 [14, 28, 24, 128], P('gx', 'gy', 'gz')
Inputs may be any that keep to these rules, and one draw needn't show every extreme that they name: `orient_flip`: 1 reverses the orientation of that degree of freedom in that element, 0 keeps it.
All inputs are finite; a program needn't handle non-finite values.
Results may differ from a plain program's by a relative error of at most 0.00007.
Values sent between devices are 32-bit elements; how exact they have to be, the bound alone decides.
A program may use at most 64 MiB of HBM per device.

v0:
```python
import functools
import jax
import jax.numpy as jnp
import numpy as np
from jax import lax
from jax.experimental import pallas as pl
from jax.experimental.pallas import tpu as pltpu
from jax.sharding import PartitionSpec as P

ORDER = 3
QUAD = 4
ELEM_DOFS = 144
QPTS = 64
AXES = ("gx", "gy", "gz")
MESH = pl.DeviceIdType.MESH
VMEM_ALL = 67043328


def lagrange(points_at, evaluate_at):
    amount = len(points_at)
    values = np.ones((len(evaluate_at), amount))
    slopes = np.zeros((len(evaluate_at), amount))
    for which in range(amount):
        for column in range(amount):
            if column != which:
                factor = (evaluate_at - points_at[column]) / (points_at[which] - points_at[column])
                slopes[:, which] = slopes[:, which] * factor + values[:, which] / (
                    points_at[which] - points_at[column]
                )
                values[:, which] = values[:, which] * factor
    return (values, slopes)


def basis_tables():
    lobatto = np.array([0.0, (1 - 5 ** (-0.5)) / 2, (1 + 5 ** (-0.5)) / 2, 1.0])
    gauss_open = np.array([(1 - 0.6**0.5) / 2, 0.5, (1 + 0.6**0.5) / 2])
    inner_pt = (3.0 / 7 - 2.0 / 7 * (6.0 / 5) ** 0.5) ** 0.5
    outer_pt = (3.0 / 7 + 2.0 / 7 * (6.0 / 5) ** 0.5) ** 0.5
    inner_wt = (18 + 30**0.5) / 36
    outer_wt = (18 - 30**0.5) / 36
    quad_points = (1 + np.array([-outer_pt, -inner_pt, inner_pt, outer_pt])) / 2
    quad_weight = np.array([outer_wt, inner_wt, inner_wt, outer_wt]) / 2
    closed, _ = lagrange(lobatto, quad_points)
    opened, _ = lagrange(gauss_open, quad_points)
    _, colloc = lagrange(quad_points, quad_points)
    return closed, opened, colloc, quad_weight


CLOSED, OPENED, COLLOC, WEIGHT = basis_tables()


def add_all(terms):
    total = terms[0]
    for term in terms[1:]:
        total = total + term
    return total


def apply(mat, xs, sigma=1):
    rows, cols = mat.shape
    half = cols // 2
    plus = [xs[p] + xs[cols - 1 - p] for p in range(half)]
    minus = [xs[p] - xs[cols - 1 - p] for p in range(half)]
    ys = [None] * rows
    for q in range((rows + 1) // 2):
        even_c = [(mat[q, p] + mat[q, cols - 1 - p]) / 2 for p in range(half)]
        odd_c = [(mat[q, p] - mat[q, cols - 1 - p]) / 2 for p in range(half)]
        even = [np.float32(c) * s for c, s in zip(even_c, plus)]
        if cols % 2:
            even.append(np.float32(mat[q, half]) * xs[half])
        even = add_all(even)
        if 2 * q == rows - 1:
            ys[q] = even
            continue
        odd = add_all([np.float32(c) * d for c, d in zip(odd_c, minus)])
        ys[q] = even + odd
        ys[rows - 1 - q] = even - odd if sigma > 0 else odd - even
    return ys


def swap(blocks, size):
    count = blocks[0].shape[0] // size
    return [
        jnp.concatenate([b[q * size : (q + 1) * size] for b in blocks], 0) for q in range(count)
    ]


def dims_of(comp):
    return [ORDER if axis == comp else ORDER + 1 for axis in range(3)]


def kernel(
    mesh_sizes, vec_hbm, flip_hbm, reluct_hbm, conduct_hbm, out_x, out_y, out_z,
    vec, flip, reluct, conduct, elem, sign, mass, curlw, flat, tmp, uq, cq,
    res_x, res_y, res_z, pack1, corner1, hx, hy, hz, hc, pack2_x, pack2_y, pack2_z, corner2,
    near_x, near_y, near_z, last_x, last_y, last_z, rc,
    s1, r1, s2, r2, s0,
):
    f32 = jnp.float32
    cx, cy = flip.shape[0], flip.shape[1]
    cz = flip.shape[2] // ELEM_DOFS
    counts = (cx, cy, cz)
    ne = cx * cy * cz
    size = tuple(ORDER * c for c in counts)
    me = [lax.axis_index(a) for a in AXES]

    def device(shift):
        return tuple(
            lax.rem(me[a] + (shift[a] + mesh_sizes[a]), mesh_sizes[a]) for a in range(3)
        )

    offsets = []
    for dx in (-1, 0, 1):
        for dy in (-1, 0, 1):
            for dz in (-1, 0, 1):
                if 1 <= abs(dx) + abs(dy) + abs(dz) <= 2:
                    offsets.append((dx, dy, dz))
    fetches = [
        pltpu.make_async_copy(src, dst, s0.at[t])
        for t, (src, dst) in enumerate(
            ((vec_hbm, vec), (flip_hbm, flip), (reluct_hbm, reluct), (conduct_hbm, conduct))
        )
    ]
    for fetch in fetches:
        fetch.start()
    barrier = pltpu.get_barrier_semaphore()
    for shift in offsets:
        pl.semaphore_signal(barrier, inc=1, device_id=device(shift), device_id_type=MESH)

    fetches[0].wait()
    for comp in (0, 1):
        for x in range(size[0]):
            for y in range(size[1]):
                pack1[comp, x, y : y + 1, :] = vec[comp, x, y, 0:1, :]
    for x in range(size[0]):
        corner1[0, x : x + 1, :] = vec[0, x, 0, 0:1, :]
    for y in range(size[1]):
        corner1[1, y : y + 1, :] = vec[1, 0, y, 0:1, :]
    pl.semaphore_wait(barrier, len(offsets))

    def send(src, dst, shift, sends, recvs, which):
        copy = pltpu.make_async_remote_copy(
            src_ref=src, dst_ref=dst, send_sem=sends.at[which], recv_sem=recvs.at[which],
            device_id=device(shift), device_id_type=MESH,
        )
        copy.start()
        return copy

    one = [
        send(corner1.at[0], hc.at[0], (0, -1, -1), s1, r1, 4),
        send(vec.at[2, 0, 0], hc.at[2], (-1, -1, 0), s1, r1, 6),
        send(corner1.at[1], hc.at[1], (-1, 0, -1), s1, r1, 5),
        send(vec.at[0, :, 0], hy.at[0], (0, -1, 0), s1, r1, 0),
        send(vec.at[2, :, 0], hy.at[1], (0, -1, 0), s1, r1, 1),
        send(pack1, hz, (0, 0, -1), s1, r1, 3),
        send(vec.at[1:3, 0], hx, (-1, 0, 0), s1, r1, 2),
    ]

    for fetch in fetches[1:]:
        fetch.wait()
    for i in range(cx):
        for j in range(cy):
            for k in range(cz):
                e = (i * cy + j) * cz + k
                flat[0, e : e + 1, 0:ELEM_DOFS] = 1.0 - 2.0 * flip[
                    i, j : j + 1, k * ELEM_DOFS : (k + 1) * ELEM_DOFS
                ].astype(f32)
                flat[1, e : e + 1, 0:QPTS] = reluct[i, j : j + 1, k * QPTS : (k + 1) * QPTS]
                flat[2, e : e + 1, 0:QPTS] = conduct[i, j : j + 1, k * QPTS : (k + 1) * QPTS]
    lanes = vec.shape[-1]
    for d in range(ELEM_DOFS):
        sign[d * ne : (d + 1) * ne, :] = jnp.broadcast_to(flat[0, :, d : d + 1], (ne, lanes))
    for q in range(QPTS):
        w = np.float32(WEIGHT[q // 16] * WEIGHT[q // 4 % 4] * WEIGHT[q % 4])
        rows = slice(q * ne, (q + 1) * ne)
        curlw[rows, :] = jnp.broadcast_to(flat[1, :, q : q + 1] * w, (ne, lanes))
        mass[rows, :] = jnp.broadcast_to(flat[2, :, q : q + 1] * w, (ne, lanes))

    def homes(comp, axis, low, high):
        found = []
        for el in range(counts[axis]):
            first = max(low, ORDER * el)
            last = min(high, ORDER * el + dims_of(comp)[axis])
            if first < last:
                found.append((el, first - ORDER * el, first - low, last - first))
        return found

    def places(comp, axis, at, low, high):
        dims = dims_of(comp)
        steps = (dims[1] * dims[2], dims[2], 1)
        span = [(p, p + 1) for p in at]
        span[axis] = (low, high)
        for fx in homes(comp, 0, *span[0]):
            for fy in homes(comp, 1, *span[1]):
                for fz in homes(comp, 2, *span[2]):
                    found = (fx, fy, fz)
                    e = (fx[0] * cy + fy[0]) * cz + fz[0]
                    d = comp * 48 + sum(found[t][1] * steps[t] for t in range(3))
                    yield found[axis][2], found[axis][3], d * ne + e, steps[axis] * ne

    def put(comp, axis, at, low, high, load):
        for offset, length, row, stride in places(comp, axis, at, low, high):
            elem[pl.ds(row, length, stride=stride), :] = load(offset, offset + length)

    for comp in range(3):
        for x in range(size[0]):
            for y in range(size[1]):
                put(comp, 2, (x, y, 0), 0, size[2], lambda a, b: vec[comp, x, y, a:b, :])

    def take_halo(comp):
        if comp == 1:
            for which in (2, 5, 6):
                one[which].wait_recv()
            for y in range(size[1]):
                put(1, 2, (size[0], y, 0), 0, size[2], lambda a, b: hx[0, y, a:b, :])
            for x in range(size[0]):
                put(1, 1, (x, 0, size[2]), 0, size[1], lambda a, b: hz[1, x, a:b, :])
            put(1, 1, (size[0], 0, size[2]), 0, size[1], lambda a, b: hc[1, a:b, :])
        elif comp == 0:
            for which in (0, 3):
                one[which].wait_recv()
            for x in range(size[0]):
                put(0, 2, (x, size[1], 0), 0, size[2], lambda a, b: hy[0, x, a:b, :])
                put(0, 1, (x, 0, size[2]), 0, size[1], lambda a, b: hz[0, x, a:b, :])
            put(0, 0, (0, size[1], size[2]), 0, size[0], lambda a, b: hc[0, a:b, :])
        else:
            for which in (1, 4):
                one[which].wait_recv()
            for x in range(size[0]):
                put(2, 2, (x, size[1], 0), 0, size[2], lambda a, b: hy[1, x, a:b, :])
            for y in range(size[1]):
                put(2, 2, (size[0], y, 0), 0, size[2], lambda a, b: hx[1, y, a:b, :])
            put(2, 2, (size[0], size[1], 0), 0, size[2], lambda a, b: hc[2, a:b, :])

    def rows_of(axis, at, line, dims):
        others = [t for t in range(3) if t != axis]
        points = []
        for last in range(dims[others[1]]):
            index = [0, 0, 0]
            index[axis], index[others[0]], index[others[1]] = at, line, last
            points.append(((index[0] * dims[1] + index[1]) * dims[2] + index[2]) * ne)
        return points

    def load_line(ref, base, axis, at, line, dims):
        starts = [base + r for r in rows_of(axis, at, line, dims)]
        if len(starts) > 1 and starts[1] - starts[0] == ne:
            return ref[starts[0] : starts[-1] + ne, :]
        return jnp.concatenate([ref[s : s + ne, :] for s in starts], 0)

    def load_plane(ref, base, axis, at, dims):
        others = [t for t in range(3) if t != axis]
        return [load_line(ref, base, axis, at, p, dims) for p in range(dims[others[0]])]

    def store_plane(ref, base, axis, at, dims, blocks):
        for p, block in enumerate(blocks):
            starts = [base + r for r in rows_of(axis, at, p, dims)]
            if starts[1] - starts[0] == ne:
                ref[starts[0] : starts[-1] + ne, :] = block
            else:
                for t, s in enumerate(starts):
                    ref[s : s + ne, :] = block[t * ne : (t + 1) * ne]

    full = [QUAD] * 3

    def mid_dims(comp):
        return [ORDER if axis == comp else QUAD for axis in range(3)]

    for comp in (1, 0, 2):
        take_halo(comp)
        dims = dims_of(comp)
        base = comp * 48 * ne
        for a in range(ORDER):
            plane = load_plane(elem, base, comp, a, dims)
            signs = load_plane(sign, base, comp, a, dims)
            plane = [p * s for p, s in zip(plane, signs)]
            plane = apply(CLOSED, plane)
            plane = apply(CLOSED, swap(plane, ne))
            store_plane(tmp, base, comp, a, mid_dims(comp), swap(plane, ne))
        others = [t for t in range(3) if t != comp]
        for line in range(QUAD):
            xs = [load_line(tmp, base, comp, a, line, mid_dims(comp)) for a in range(ORDER)]
            for q, y in enumerate(apply(OPENED, xs)):
                starts = [comp * 64 * ne + r for r in rows_of(comp, q, line, full)]
                if starts[1] - starts[0] == ne:
                    uq[starts[0] : starts[-1] + ne, :] = y
                else:
                    for t, s in enumerate(starts):
                        uq[s : s + ne, :] = y[t * ne : (t + 1) * ne]

    part = 64 * ne

    for c in range(3):
        p, r = [t for t in range(3) if t != c]
        flipped = -1 if c == 1 else 1
        for at in range(QUAD):
            u_p = load_plane(uq, p * part, c, at, full)
            u_r = load_plane(uq, r * part, c, at, full)
            along_p = apply(COLLOC, u_r, -1)
            along_r = swap(apply(COLLOC, swap(u_p, ne), -1), ne)
            if flipped > 0:
                curl = [f - g for f, g in zip(along_p, along_r)]
            else:
                curl = [g - f for f, g in zip(along_p, along_r)]
            scale = load_plane(curlw, 0, c, at, full)
            store_plane(cq, c * part, c, at, full, [k * w for k, w in zip(curl, scale)])

    closed_t, opened_t, colloc_t = CLOSED.T, OPENED.T, COLLOC.T
    results = (res_x, res_y, res_z)
    packs = (pack2_x, pack2_y, pack2_z)
    near = (near_x, near_y, near_z)
    last = (last_x, last_y, last_z)
    orders = ((0, 1, 2), (0, 1, 2), (0, 2, 1))
    sends = {}
    for res in results:
        res[...] = jnp.zeros_like(res)
    for comp in (0, 2, 1):
        dims = dims_of(comp)
        base = comp * 48 * ne
        p, r = [t for t in range(3) if t != comp]
        for at in range(QUAD):
            u = load_plane(uq, comp * part, comp, at, full)
            m = load_plane(mass, 0, comp, at, full)
            total = [a * b for a, b in zip(u, m)]
            by_p = apply(colloc_t, load_plane(cq, r * part, comp, at, full), -1)
            by_r = apply(colloc_t, swap(load_plane(cq, p * part, comp, at, full), ne), -1)
            by_r = swap(by_r, ne)
            if comp == 1:
                total = [t + a - b for t, a, b in zip(total, by_p, by_r)]
            else:
                total = [t - a + b for t, a, b in zip(total, by_p, by_r)]
            total = apply(closed_t, total)
            total = apply(closed_t, swap(total, ne))
            kept = [QUAD if axis == comp else ORDER + 1 for axis in range(3)]
            store_plane(tmp, 0, comp, at, kept, swap(total, ne))
        for line in range(ORDER + 1):
            xs = [load_line(tmp, 0, comp, q, line, kept) for q in range(QUAD)]
            for a, y in enumerate(apply(opened_t, xs)):
                y = y * load_line(sign, base, comp, a, line, dims)
                for t, s in enumerate(rows_of(comp, a, line, dims)):
                    elem[base + s : base + s + ne, :] = y[t * ne : (t + 1) * ne]
        res = results[comp]
        order = orders[comp]
        for first in range(res.shape[0]):
            for middle in range(res.shape[1]):
                at = [0, 0, 0]
                at[order[0]], at[order[1]] = first, middle
                pieces = places(comp, order[2], at, 0, res.shape[2])
                for offset, length, row, stride in pieces:
                    res[first, middle, offset : offset + length, :] += elem[
                        pl.ds(row, length, stride=stride), :
                    ]
        rim = order[1] if comp == 0 else order[0]
        open_size, rim_size, last_size = size[comp], size[rim], size[order[2]]
        copies = []
        for s_rim in (0, 1):
            for s_last in (0, 1):
                shift = [0, 0, 0]
                shift[rim], shift[order[2]] = 2 * s_rim - 1, 2 * s_last - 1
                slot = 2 * s_rim + s_last
                where = 4 * comp + slot
                edge, row = s_rim * rim_size, s_last * last_size
                for t in range(open_size):
                    f, m = (t, edge) if comp == 0 else (edge, t)
                    corner2[where, t : t + 1, :] = res[f, m, row : row + 1, :]
                copies.append(
                    send(corner2.at[where], rc.at[where], shift, s2, r2, 8 * comp + slot)
                )
        for side in (0, 1):
            shift = [0, 0, 0]
            shift[rim] = 2 * side - 1
            edge = side * rim_size
            src = res.at[:, edge] if comp == 0 else res.at[edge]
            copies.append(send(src, near[comp].at[side], shift, s2, r2, 8 * comp + 4 + side))
        for side in (0, 1):
            shift = [0, 0, 0]
            shift[order[2]] = 2 * side - 1
            row = side * last_size
            for f in range(res.shape[0]):
                for m in range(res.shape[1]):
                    packs[comp][side, f, m : m + 1, :] = res[f, m, row : row + 1, :]
            copies.append(
                send(packs[comp].at[side], last[comp].at[side], shift, s2, r2, 8 * comp + 6 + side)
            )
        sends[comp] = copies

    outs = (out_x, out_y, out_z)
    for comp in range(3):
        outs[comp][...] = results[comp][...]
    for comp in (1, 0, 2):
        out, order = outs[comp], orders[comp]
        rim = order[1] if comp == 0 else order[0]
        for copy in sends[comp]:
            copy.wait_recv()
        for side in (0, 1):
            edge = (1 - side) * size[rim]
            row = (1 - side) * size[order[2]]
            if comp == 0:
                for f in range(out.shape[0]):
                    out[f, edge] += near[comp][side, f]
            else:
                out[edge] += near[comp][side]
            for f in range(out.shape[0]):
                for m in range(out.shape[1]):
                    out[f, m, row : row + 1, :] += last[comp][side, f, m : m + 1, :]
            for s_last in (0, 1):
                where = 4 * comp + 2 * side + s_last
                row = (1 - s_last) * size[order[2]]
                for t in range(size[comp]):
                    f, m = (t, edge) if comp == 0 else (edge, t)
                    out[f, m, row : row + 1, :] += rc[where, t : t + 1, :]
    for copy in one + sends[0] + sends[1] + sends[2]:
        copy.wait_send()


def write_out(from_x, from_y, from_z, to_x, to_y, to_z, sems):
    pairs = ((from_x, to_x), (from_y, to_y), (from_z, to_z))
    copies = [pltpu.make_async_copy(src, dst, sems.at[t]) for t, (src, dst) in enumerate(pairs)]
    for copy in copies:
        copy.start()
    for copy in copies:
        copy.wait()


def on_device(mesh_sizes, vectors, orient_flip, reluctivity, conductivity):
    counts = (
        orient_flip.shape[0], orient_flip.shape[1], orient_flip.shape[2] // ELEM_DOFS,
    )
    ne = counts[0] * counts[1] * counts[2]
    sx, sy, sz = (ORDER * c for c in counts)
    lanes = vectors.shape[-1]
    f32 = jnp.float32
    shapes = (
        (sx, sy + 1, sz + 1, lanes), (sx + 1, sy, sz + 1, lanes), (sx + 1, sz, sy + 1, lanes),
    )
    longest = max(sx, sy, sz)
    faces = tuple((2,) + s[:2] + (lanes,) for s in shapes)
    scratch = [
        (ELEM_DOFS * ne, lanes), (ELEM_DOFS * ne, lanes), (QPTS * ne, lanes), (QPTS * ne, lanes),
        (3, ne, ELEM_DOFS), (ELEM_DOFS * ne, lanes), (3 * QPTS * ne, lanes), (3 * QPTS * ne, lanes),
        *shapes,
        (2, sx, sy, lanes), (2, longest, lanes),
        (2, sy, sz, lanes), (2, sx, sz, lanes), (2, sx, sy, lanes), (3, longest, lanes),
        *faces, (12, longest, lanes),
        (2, sx, sz + 1, lanes), (2, sy, sz + 1, lanes), (2, sz, sy + 1, lanes),
        *faces, (12, longest, lanes),
    ]
    vmem = pl.BlockSpec(memory_space=pltpu.VMEM)
    padded = [s[0] * s[1] * (s[2] + -s[2] % 8) * lanes * 4 for s in shapes]
    room = sum(padded) + max(padded)
    anywhere = pl.BlockSpec(memory_space=pltpu.HBM)
    arguments = (vectors, orient_flip, reluctivity, conductivity)
    outs = [jax.ShapeDtypeStruct(s, f32) for s in shapes]
    held = pl.pallas_call(
        functools.partial(kernel, mesh_sizes),
        out_shape=[pltpu.VMEM(s, f32) for s in shapes],
        in_specs=[anywhere] * 4,
        out_specs=[vmem] * 3,
        scratch_shapes=[pltpu.VMEM(a.shape, a.dtype) for a in arguments]
        + [pltpu.VMEM(s, f32) for s in scratch]
        + [pltpu.SemaphoreType.DMA((7,))] * 2
        + [pltpu.SemaphoreType.DMA((24,))] * 2
        + [pltpu.SemaphoreType.DMA((4,))],
        compiler_params=pltpu.CompilerParams(
            collective_id=0, has_side_effects=True, vmem_limit_bytes=VMEM_ALL - room
        ),
        name="curl_mass",
    )(*arguments)
    held = pl.pallas_call(
        write_out,
        out_shape=outs,
        in_specs=[pl.BlockSpec(memory_space=pl.ANY)] * 3,
        out_specs=[anywhere] * 3,
        scratch_shapes=[pltpu.SemaphoreType.DMA((3,))],
        compiler_params=pltpu.CompilerParams(vmem_limit_bytes=2**20),
        name="write_out",
    )(*held)
    return held[0], held[1], jnp.swapaxes(held[2], 1, 2)


def solution(mesh):
    return jax.shard_map(
        functools.partial(on_device, tuple(mesh.shape[a] for a in AXES)),
        mesh=mesh,
        in_specs=(
            P(None, "gx", "gy", "gz", None),
            P("gx", "gy", "gz"),
            P("gx", "gy", "gz"),
            P("gx", "gy", "gz"),
        ),
        out_specs=(P("gx", "gy", "gz", None), P("gx", "gy", "gz", None), P("gx", "gy", "gz", None)),
        check_vma=False,
    )
```

profile of v0, /device:TPU:0, one launch (start us, length us, event | category | flops | bytes accessed | tf_op | source)
XLA Modules:
  0.0 18.6 jit_solution(7885236861628514574)
XLA Ops:
  0.6 17.2 %curl_mass.1 = (f32[6,7,7,128]{3,2,1,0:T(8,128)S(1)}, f32[7,6,7,128]{3,2,1,0:T(8,128)S(1)}, f32[7,6,7,128]{3,2,1,0:T(8,128)S(1)}) custom-call(f32[3,6,6,6,128]{4,3,2,1,0:T(8,128)} %vec_hbm.1, s32[2,2,288]{2,1,0:T(2,128)} %flip_hbm.1, f32[2,2,128]{2,1,0:T(2,128)} %reluct_hbm.1, f32[2,2,128]{2,1,0:T(2,128)} %conduct_hbm.1), custom_call_target="tpu_custom_call" | custom-call | tf_op jit(solution)/shard_map/curl_mass/pallas_call | solution.py:453
  17.8 0.8 %write_out.1 = (f32[6,7,7,128]{3,2,1,0:T(8,128)}, f32[7,6,7,128]{3,2,1,0:T(8,128)}, f32[7,6,7,128]{3,2,1,0:T(8,128)}) custom-call(f32[6,7,7,128]{3,2,1,0:T(8,128)S(1)} %get-tuple-element.9.from_x, f32[7,6,7,128]{3,2,1,0:T(8,128)S(1)} %get-tuple-element.10.from_y, f32[7,6,7,128]{3,2,1,0:T(8,128)S(1)} %get-tuple-element.11.from_z), custom_call_target="tpu_custom_call" | custom-call | tf_op jit(solution)/shard_map/write_out/pallas_call | solution.py:468
where the time goes:
time: 18.8 us; the launch traced here: 18.6 us
  Pallas kernels  18 us (96%)
  between operations  0.64 us (3%)
    pallas_call x1, Pallas kernels, on_device(): pl.pallas_call(functools.partial(kernel, mesh_sizes), out_shape=[pltpu.VM...  17.2 us
    pallas_call x1, Pallas kernels, on_device(): pl.pallas_call(write_out, out_shape=outs, in_specs=[pl.BlockSpec(memory_s...  0.79 us

commit v1 on v0

--- a/solution.py
+++ b/solution.py
@@ -94,7 +94,8 @@
     vec, flip, reluct, conduct, elem, sign, mass, curlw, flat, tmp, uq, cq,
     res_x, res_y, res_z, pack1, corner1, hx, hy, hz, hc, pack2_x, pack2_y, pack2_z, corner2,
     near_x, near_y, near_z, last_x, last_y, last_z, rc,
-    s1, r1, s2, r2, s0,
+    face, face_own, face_out, coef, coef_in, top_x, top_z, low_x,
+    s1, r1, s2, r2, s0, ready,
 ):
     f32 = jnp.float32
     cx, cy = flip.shape[0], flip.shape[1]
@@ -102,6 +103,7 @@
     counts = (cx, cy, cz)
     ne = cx * cy * cz
     size = tuple(ORDER * c for c in counts)
+    lanes = vec.shape[-1]
     me = [lax.axis_index(a) for a in AXES]
 
     def device(shift):
@@ -109,12 +111,9 @@
             lax.rem(me[a] + (shift[a] + mesh_sizes[a]), mesh_sizes[a]) for a in range(3)
         )
 
-    offsets = []
-    for dx in (-1, 0, 1):
-        for dy in (-1, 0, 1):
-            for dz in (-1, 0, 1):
-                if 1 <= abs(dx) + abs(dy) + abs(dz) <= 2:
-                    offsets.append((dx, dy, dz))
+    def signal(sem, shift):
+        pl.semaphore_signal(sem, inc=1, device_id=device(shift), device_id_type=MESH)
+
     fetches = [
         pltpu.make_async_copy(src, dst, s0.at[t])
         for t, (src, dst) in enumerate(
@@ -124,8 +123,11 @@
     for fetch in fetches:
         fetch.start()
     barrier = pltpu.get_barrier_semaphore()
-    for shift in offsets:
-        pl.semaphore_signal(barrier, inc=1, device_id=device(shift), device_id_type=MESH)
+    greeted = (
+        (0, -1, 0), (1, 0, 0), (0, 0, 1), (1, 0, 1), (1, -1, 0), (-1, -1, 0), (0, -1, 1), (0, -1, -1),
+    )
+    for shift in greeted:
+        signal(barrier, shift)
 
     fetches[0].wait()
     for comp in (0, 1):
@@ -136,7 +138,7 @@
         corner1[0, x : x + 1, :] = vec[0, x, 0, 0:1, :]
     for y in range(size[1]):
         corner1[1, y : y + 1, :] = vec[1, 0, y, 0:1, :]
-    pl.semaphore_wait(barrier, len(offsets))
+    pl.semaphore_wait(barrier, len(greeted))
 
     def send(src, dst, shift, sends, recvs, which):
         copy = pltpu.make_async_remote_copy(
@@ -146,15 +148,13 @@
         copy.start()
         return copy
 
-    one = [
-        send(corner1.at[0], hc.at[0], (0, -1, -1), s1, r1, 4),
-        send(vec.at[2, 0, 0], hc.at[2], (-1, -1, 0), s1, r1, 6),
-        send(corner1.at[1], hc.at[1], (-1, 0, -1), s1, r1, 5),
-        send(vec.at[0, :, 0], hy.at[0], (0, -1, 0), s1, r1, 0),
-        send(vec.at[2, :, 0], hy.at[1], (0, -1, 0), s1, r1, 1),
-        send(pack1, hz, (0, 0, -1), s1, r1, 3),
-        send(vec.at[1:3, 0], hx, (-1, 0, 0), s1, r1, 2),
-    ]
+    one = {
+        2: send(vec.at[1:3, 0], hx, (-1, 0, 0), s1, r1, 2),
+        5: send(corner1.at[1], hc.at[1], (-1, 0, -1), s1, r1, 5),
+        3: send(pack1, hz, (0, 0, -1), s1, r1, 3),
+    }
+    for shift in ((0, 1, 0), (1, 1, 0), (-1, 1, 0), (0, 1, 1), (0, 1, -1)):
+        signal(ready, shift)
 
     for fetch in fetches[1:]:
         fetch.wait()
@@ -167,7 +167,6 @@
                 ].astype(f32)
                 flat[1, e : e + 1, 0:QPTS] = reluct[i, j : j + 1, k * QPTS : (k + 1) * QPTS]
                 flat[2, e : e + 1, 0:QPTS] = conduct[i, j : j + 1, k * QPTS : (k + 1) * QPTS]
-    lanes = vec.shape[-1]
     for d in range(ELEM_DOFS):
         sign[d * ne : (d + 1) * ne, :] = jnp.broadcast_to(flat[0, :, d : d + 1], (ne, lanes))
     for q in range(QPTS):
@@ -175,6 +174,35 @@
         rows = slice(q * ne, (q + 1) * ne)
         curlw[rows, :] = jnp.broadcast_to(flat[1, :, q : q + 1] * w, (ne, lanes))
         mass[rows, :] = jnp.broadcast_to(flat[2, :, q : q + 1] * w, (ne, lanes))
+
+    line_c, line_s = CLOSED[:, ORDER], COLLOC @ CLOSED[:, ORDER]
+    face_dofs = [(a * 4 + 3) * 4 + c for a in range(3) for c in range(4)]
+    face_dofs += [96 + (a * 4 + 3) * 3 + c for a in range(4) for c in range(3)]
+
+    def quad_rows(ref, base, qx, qy):
+        first = base + (qx * 16 + qy * 4) * ne
+        return ref[first : first + 4 * ne, :]
+
+    def pieces_of(block):
+        return [block[t * ne : (t + 1) * ne] for t in range(block.shape[0] // ne)]
+
+    summed = []
+    for qx in range(QUAD):
+        summed += pieces_of(add_all(
+            [np.float32(line_c[qy] ** 2) * quad_rows(mass, 0, qx, qy) for qy in range(QUAD)]
+            + [np.float32(line_s[qy] ** 2) * quad_rows(curlw, 0, qx, qy) for qy in range(QUAD)]
+        ))
+    for qx in range(QUAD):
+        summed += pieces_of(add_all(
+            [np.float32(line_c[qy] ** 2) * quad_rows(curlw, 0, qx, qy) for qy in range(QUAD)]
+        ))
+    summed += [sign[d * ne : (d + 1) * ne, :] for d in face_dofs]
+    lane = lax.broadcasted_iota(jnp.int32, (ne, lanes), 1)
+    packed = jnp.zeros((ne, lanes), f32)
+    for t, value in enumerate(summed):
+        packed = jnp.where(lane == t, value, packed)
+    coef[...] = packed
+    one[7] = send(coef, coef_in, (0, 1, 0), s1, r1, 7)
 
     def homes(comp, axis, low, high):
         found = []
@@ -202,14 +230,44 @@
         for offset, length, row, stride in places(comp, axis, at, low, high):
             elem[pl.ds(row, length, stride=stride), :] = load(offset, offset + length)
 
+    def face_places(comp, x, low, high):
+        for fx in homes(comp, 0, x, x + 1):
+            for fz in homes(comp, 2, low, high):
+                e = (fx[0] * cy + cy - 1) * cz + fz[0]
+                d = comp // 2 * 12 + fx[1] * dims_of(comp)[2] + fz[1]
+                yield fz[2], fz[3], d * ne + e
+
+    def put_face(ref, comp, x, low, high, load):
+        for offset, length, row in face_places(comp, x, low, high):
+            ref[pl.ds(row, length, stride=ne), :] = load(offset, offset + length)
+
+    blank = jnp.zeros((ne, lanes), f32)
+    for t, d in enumerate(face_dofs):
+        elem[d * ne : (d + 1) * ne, :] = blank
+        face[t * ne : (t + 1) * ne, :] = blank
+        face_own[t * ne : (t + 1) * ne, :] = blank
     for comp in range(3):
         for x in range(size[0]):
             for y in range(size[1]):
                 put(comp, 2, (x, y, 0), 0, size[2], lambda a, b: vec[comp, x, y, a:b, :])
+    for comp in (0, 2):
+        for x in range(size[0]):
+            put_face(face_own, comp, x, 0, size[2], lambda a, b: vec[comp, x, 0, a:b, :])
+    top_x[...] = jnp.zeros_like(top_x)
+    top_z[...] = jnp.zeros_like(top_z)
+    results = (res_x, res_y, res_z)
+    for res in results:
+        res[...] = jnp.zeros_like(res)
+
+    pl.semaphore_wait(ready, 5)
+    one[4] = send(corner1.at[0], hc.at[0], (0, -1, -1), s1, r1, 4)
+    one[6] = send(vec.at[2, 0, 0], hc.at[2], (-1, -1, 0), s1, r1, 6)
+    one[0] = send(vec.at[0, :, 0], hy.at[0], (0, -1, 0), s1, r1, 0)
+    one[1] = send(vec.at[2, :, 0], hy.at[1], (0, -1, 0), s1, r1, 1)
 
     def take_halo(comp):
         if comp == 1:
-            for which in (2, 5, 6):
+            for which in (2, 5, 3):
                 one[which].wait_recv()
             for y in range(size[1]):
                 put(1, 2, (size[0], y, 0), 0, size[2], lambda a, b: hx[0, y, a:b, :])
@@ -217,20 +275,13 @@
                 put(1, 1, (x, 0, size[2]), 0, size[1], lambda a, b: hz[1, x, a:b, :])
             put(1, 1, (size[0], 0, size[2]), 0, size[1], lambda a, b: hc[1, a:b, :])
         elif comp == 0:
-            for which in (0, 3):
-                one[which].wait_recv()
             for x in range(size[0]):
-                put(0, 2, (x, size[1], 0), 0, size[2], lambda a, b: hy[0, x, a:b, :])
                 put(0, 1, (x, 0, size[2]), 0, size[1], lambda a, b: hz[0, x, a:b, :])
-            put(0, 0, (0, size[1], size[2]), 0, size[0], lambda a, b: hc[0, a:b, :])
+                put_face(face_own, 0, x, size[2], size[2] + 1, lambda a, b: hz[0, x, 0:1, :])
         else:
-            for which in (1, 4):
-                one[which].wait_recv()
-            for x in range(size[0]):
-                put(2, 2, (x, size[1], 0), 0, size[2], lambda a, b: hy[1, x, a:b, :])
             for y in range(size[1]):
                 put(2, 2, (size[0], y, 0), 0, size[2], lambda a, b: hx[1, y, a:b, :])
-            put(2, 2, (size[0], size[1], 0), 0, size[2], lambda a, b: hc[2, a:b, :])
+            put_face(face_own, 2, size[0], 0, size[2], lambda a, b: hx[1, 0, a:b, :])
 
     def rows_of(axis, at, line, dims):
         others = [t for t in range(3) if t != axis]
@@ -305,15 +356,102 @@
             store_plane(cq, c * part, c, at, full, [k * w for k, w in zip(curl, scale)])
 
     closed_t, opened_t, colloc_t = CLOSED.T, OPENED.T, COLLOC.T
-    results = (res_x, res_y, res_z)
     packs = (pack2_x, pack2_y, pack2_z)
     near = (near_x, near_y, near_z)
     last = (last_x, last_y, last_z)
     orders = ((0, 1, 2), (0, 1, 2), (0, 2, 1))
-    sends = {}
-    for res in results:
-        res[...] = jnp.zeros_like(res)
-    for comp in (0, 2, 1):
+    sends = {0: [], 1: [], 2: []}
+
+    def face_values(ref, signs):
+        at = [ref[t * ne : (t + 1) * ne, :] * signs[t] for t in range(24)]
+        xs = [jnp.concatenate([at[a * 4 + c] for a in range(3)], 0) for c in range(4)]
+        u_x = apply(OPENED, swap(apply(CLOSED, xs), ne))
+        xs = [jnp.concatenate([at[12 + a * 3 + c] for c in range(3)], 0) for a in range(4)]
+        u_z = swap(apply(OPENED, swap(apply(CLOSED, xs), ne)), ne)
+        along_z = swap(apply(COLLOC, swap(u_x, ne), -1), ne)
+        along_x = apply(COLLOC, u_z, -1)
+        return u_x, u_z, [f - g for f, g in zip(along_z, along_x)]
+
+    def face_gradient(v_x, v_z, b, signs):
+        by_z = swap(apply(colloc_t, swap(b, ne), -1), ne)
+        by_x = apply(colloc_t, b, -1)
+        v_x = [v + f for v, f in zip(v_x, by_z)]
+        v_z = [v - f for v, f in zip(v_z, by_x)]
+        for c, block in enumerate(apply(closed_t, swap(apply(opened_t, v_x), ne))):
+            for a, y in enumerate(pieces_of(block)):
+                t = a * 4 + c
+                face_out[t * ne : (t + 1) * ne, :] = y * signs[t]
+        for c, block in enumerate(apply(opened_t, swap(apply(closed_t, v_z), ne))):
+            for a, y in enumerate(pieces_of(block)):
+                t = 12 + a * 3 + c
+                face_out[t * ne : (t + 1) * ne, :] = y * signs[t]
+
+    v_x, v_z, b = [], [], []
+    for qx in range(QUAD):
+        t_x, t_z, t_b = [], [], []
+        for qy in range(QUAD):
+            m = quad_rows(mass, 0, qx, qy) * np.float32(line_c[qy])
+            slope = np.float32(line_s[qy])
+            t_x += [m * quad_rows(uq, 0, qx, qy), -slope * quad_rows(cq, 2 * part, qx, qy)]
+            t_z += [m * quad_rows(uq, 2 * part, qx, qy), slope * quad_rows(cq, 0, qx, qy)]
+            t_b += [np.float32(line_c[qy]) * quad_rows(cq, part, qx, qy)]
+        v_x.append(add_all(t_x))
+        v_z.append(add_all(t_z))
+        b.append(add_all(t_b))
+    own_signs = [sign[d * ne : (d + 1) * ne, :] for d in face_dofs]
+    face_gradient(v_x, v_z, b, own_signs)
+    for comp, top in ((0, top_x), (2, top_z)):
+        for x in range(top.shape[0]):
+            for offset, length, row in face_places(comp, x, 0, top.shape[1]):
+                top[x, offset : offset + length, :] += face_out[pl.ds(row, length, stride=ne), :]
+
+    def send_corner(comp, shift, slot, load):
+        where = 4 * comp + slot
+        for t in range(size[comp]):
+            corner2[where, t : t + 1, :] = load(t)
+        sends[comp].append(
+            send(corner2.at[where], rc.at[where], shift, s2, r2, 8 * comp + slot)
+        )
+
+    for s in (0, 1):
+        send_corner(0, (0, 1, 2 * s - 1), 2 + s, lambda t: top_x[t, s * size[2] : s * size[2] + 1, :])
+        send_corner(2, (2 * s - 1, 1, 0), 2 * s + 1, lambda t: top_z[s * size[0], t : t + 1, :])
+    sends[0].append(send(top_x, near_x.at[1], (0, 1, 0), s2, r2, 5))
+    sends[2].append(send(top_z, last_z.at[1], (0, 1, 0), s2, r2, 16 + 7))
+
+    for which in (0, 1, 4, 6):
+        one[which].wait_recv()
+    for x in range(size[0]):
+        put_face(face, 0, x, 0, size[2], lambda a, b: hy[0, x, a:b, :])
+        put_face(face, 0, x, size[2], size[2] + 1, lambda a, b: hc[0, x : x + 1, :])
+        put_face(face, 2, x, 0, size[2], lambda a, b: hy[1, x, a:b, :])
+    put_face(face, 2, size[0], 0, size[2], lambda a, b: hc[2, a:b, :])
+    u_x, u_z, turn = face_values(face, own_signs)
+    for qx in range(QUAD):
+        for qy in range(QUAD):
+            first = (qx * 16 + qy * 4) * ne
+            value, slope = np.float32(line_c[qy]), np.float32(line_s[qy])
+            w = curlw[first : first + 4 * ne, :]
+            sloped = w * slope
+            uq[first : first + 4 * ne, :] += value * u_x[qx]
+            uq[2 * part + first : 2 * part + first + 4 * ne, :] += value * u_z[qx]
+            cq[first : first + 4 * ne, :] += sloped * u_z[qx]
+            cq[part + first : part + first + 4 * ne, :] += (w * value) * turn[qx]
+            cq[2 * part + first : 2 * part + first + 4 * ne, :] -= sloped * u_x[qx]
+
+    for comp in (1, 0, 2):
+        if comp == 0:
+            one[7].wait_recv()
+            theirs = [
+                jnp.broadcast_to(coef_in[:, t : t + 1], (ne, lanes)) for t in range(56)
+            ]
+            u_x, u_z, turn = face_values(face_own, theirs[32:])
+            m2 = [jnp.concatenate(theirs[4 * qx : 4 * qx + 4], 0) for qx in range(QUAD)]
+            k2 = [jnp.concatenate(theirs[16 + 4 * qx : 20 + 4 * qx], 0) for qx in range(QUAD)]
+            face_gradient(
+                [m * u for m, u in zip(m2, u_x)], [m * u for m, u in zip(m2, u_z)],
+                [k * u for k, u in zip(k2, turn)], theirs[32:],
+            )
         dims = dims_of(comp)
         base = comp * 48 * ne
         p, r = [t for t in range(3) if t != comp]
@@ -351,37 +489,65 @@
                     ]
         rim = order[1] if comp == 0 else order[0]
         open_size, rim_size, last_size = size[comp], size[rim], size[order[2]]
-        copies = []
-        for s_rim in (0, 1):
-            for s_last in (0, 1):
-                shift = [0, 0, 0]
-                shift[rim], shift[order[2]] = 2 * s_rim - 1, 2 * s_last - 1
-                slot = 2 * s_rim + s_last
-                where = 4 * comp + slot
-                edge, row = s_rim * rim_size, s_last * last_size
-                for t in range(open_size):
-                    f, m = (t, edge) if comp == 0 else (edge, t)
-                    corner2[where, t : t + 1, :] = res[f, m, row : row + 1, :]
-                copies.append(
-                    send(corner2.at[where], rc.at[where], shift, s2, r2, 8 * comp + slot)
-                )
-        for side in (0, 1):
+
+        def corner(s_rim, s_last):
+            shift = [0, 0, 0]
+            shift[rim], shift[order[2]] = 2 * s_rim - 1, 2 * s_last - 1
+            edge, row = s_rim * rim_size, s_last * last_size
+
+            def load(t):
+                f, m = (t, edge) if comp == 0 else (edge, t)
+                return res[f, m, row : row + 1, :]
+
+            send_corner(comp, shift, 2 * s_rim + s_last, load)
+
+        def send_near(src, side):
             shift = [0, 0, 0]
             shift[rim] = 2 * side - 1
-            edge = side * rim_size
-            src = res.at[:, edge] if comp == 0 else res.at[edge]
-            copies.append(send(src, near[comp].at[side], shift, s2, r2, 8 * comp + 4 + side))
-        for side in (0, 1):
+            sends[comp].append(send(src, near[comp].at[side], shift, s2, r2, 8 * comp + 4 + side))
+
+        def send_last(side):
             shift = [0, 0, 0]
             shift[order[2]] = 2 * side - 1
             row = side * last_size
             for f in range(res.shape[0]):
                 for m in range(res.shape[1]):
                     packs[comp][side, f, m : m + 1, :] = res[f, m, row : row + 1, :]
-            copies.append(
+            sends[comp].append(
                 send(packs[comp].at[side], last[comp].at[side], shift, s2, r2, 8 * comp + 6 + side)
             )
-        sends[comp] = copies
+
+        if comp == 1:
+            for s_rim in (0, 1):
+                for s_last in (0, 1):
+                    corner(s_rim, s_last)
+            for side in (0, 1):
+                send_near(res.at[side * rim_size], side)
+            for side in (0, 1):
+                send_last(side)
+        elif comp == 0:
+            for s_last in (0, 1):
+                corner(0, s_last)
+            for f in range(res.shape[0]):
+                low_x[f] = res[f, 0]
+            send_near(low_x, 0)
+            for x in range(res.shape[0]):
+                for offset, length, row in face_places(0, x, 0, res.shape[2]):
+                    res[x, 0, offset : offset + length, :] += face_out[
+                        pl.ds(row, length, stride=ne), :
+                    ]
+            for side in (0, 1):
+                send_last(side)
+        else:
+            for s_rim in (0, 1):
+                corner(s_rim, 0)
+            send_last(0)
+            for x in range(res.shape[0]):
+                for offset, length, row in face_places(2, x, 0, res.shape[1]):
+                    for t in range(length):
+                        res[x, offset + t, 0:1, :] += face_out[row + t * ne : row + t * ne + 1, :]
+            for side in (0, 1):
+                send_near(res.at[side * rim_size], side)
 
     outs = (out_x, out_y, out_z)
     for comp in range(3):
@@ -408,7 +574,7 @@
                 for t in range(size[comp]):
                     f, m = (t, edge) if comp == 0 else (edge, t)
                     out[f, m, row : row + 1, :] += rc[where, t : t + 1, :]
-    for copy in one + sends[0] + sends[1] + sends[2]:
+    for copy in list(one.values()) + sends[0] + sends[1] + sends[2]:
         copy.wait_send()
 
 
@@ -443,6 +609,8 @@
         *faces, (12, longest, lanes),
         (2, sx, sz + 1, lanes), (2, sy, sz + 1, lanes), (2, sz, sy + 1, lanes),
         *faces, (12, longest, lanes),
+        (24 * ne, lanes), (24 * ne, lanes), (24 * ne, lanes), (ne, lanes), (ne, lanes),
+        (sx, sz + 1, lanes), (sx + 1, sz, lanes), (sx, sz + 1, lanes),
     ]
     vmem = pl.BlockSpec(memory_space=pltpu.VMEM)
     padded = [s[0] * s[1] * (s[2] + -s[2] % 8) * lanes * 4 for s in shapes]
@@ -457,9 +625,9 @@
         out_specs=[vmem] * 3,
         scratch_shapes=[pltpu.VMEM(a.shape, a.dtype) for a in arguments]
         + [pltpu.VMEM(s, f32) for s in scratch]
-        + [pltpu.SemaphoreType.DMA((7,))] * 2
+        + [pltpu.SemaphoreType.DMA((8,))] * 2
         + [pltpu.SemaphoreType.DMA((24,))] * 2
-        + [pltpu.SemaphoreType.DMA((4,))],
+        + [pltpu.SemaphoreType.DMA((4,)), pltpu.SemaphoreType.REGULAR],
         compiler_params=pltpu.CompilerParams(
             collective_id=0, has_side_effects=True, vmem_limit_bytes=VMEM_ALL - room
         ),

time: 18.8 us -> 16.8 us (0.89)
  Pallas kernels: 18 us -> 16 us
    pallas_call x1, Pallas kernels: 17.2 us -> 15.2 us  [on_device(): pl.pallas_call(functools.partial(kernel, mesh_sizes), out_shape=[pltpu.VM...]
where the time goes in v1:
time: 16.8 us; the launch traced here: 16.6 us
  Pallas kernels  16 us (95%)
  between operations  0.64 us (4%)
    pallas_call x1, Pallas kernels, on_device(): pl.pallas_call(functools.partial(kernel, mesh_sizes), out_shape=[pltpu.VM...  15.2 us
    pallas_call x1, Pallas kernels, on_device(): pl.pallas_call(write_out, out_shape=outs, in_specs=[pl.BlockSpec(memory_s...  0.79 us

profile of v1, /device:TPU:0, one launch (start us, length us, event | category | flops | bytes accessed | tf_op | source)
XLA Modules:
  0.0 16.6 jit_solution(6830632012184816190)
XLA Ops:
  0.6 15.2 %curl_mass.1 = (f32[6,7,7,128]{3,2,1,0:T(8,128)S(1)}, f32[7,6,7,128]{3,2,1,0:T(8,128)S(1)}, f32[7,6,7,128]{3,2,1,0:T(8,128)S(1)}) custom-call(f32[3,6,6,6,128]{4,3,2,1,0:T(8,128)} %vec_hbm.1, s32[2,2,288]{2,1,0:T(2,128)} %flip_hbm.1, f32[2,2,128]{2,1,0:T(2,128)} %reluct_hbm.1, f32[2,2,128]{2,1,0:T(2,128)} %conduct_hbm.1), custom_call_target="tpu_custom_call" | custom-call | tf_op jit(solution)/shard_map/curl_mass/pallas_call | solution.py:621
  15.8 0.8 %write_out.1 = (f32[6,7,7,128]{3,2,1,0:T(8,128)}, f32[7,6,7,128]{3,2,1,0:T(8,128)}, f32[7,6,7,128]{3,2,1,0:T(8,128)}) custom-call(f32[6,7,7,128]{3,2,1,0:T(8,128)S(1)} %get-tuple-element.9.from_x, f32[7,6,7,128]{3,2,1,0:T(8,128)S(1)} %get-tuple-element.10.from_y, f32[7,6,7,128]{3,2,1,0:T(8,128)S(1)} %get-tuple-element.11.from_z), custom_call_target="tpu_custom_call" | custom-call | tf_op jit(solution)/shard_map/write_out/pallas_call | solution.py:636

commit v2 on v1

--- a/solution.py
+++ b/solution.py
@@ -92,10 +92,10 @@
 def kernel(
     mesh_sizes, vec_hbm, flip_hbm, reluct_hbm, conduct_hbm, out_x, out_y, out_z,
     vec, flip, reluct, conduct, elem, sign, mass, curlw, flat, tmp, uq, cq,
-    res_x, res_y, res_z, pack1, corner1, hx, hy, hz, hc, pack2_x, pack2_y, pack2_z, corner2,
+    res_x, res_y, res_z, pack1, corner1, hx, hy, hz, hc, pack2_x, pack2_y, corner2,
     near_x, near_y, near_z, last_x, last_y, last_z, rc,
-    face, face_own, face_out, coef, coef_in, top_x, top_z, low_x,
-    s1, r1, s2, r2, s0, ready,
+    face, face_own, face_out, coef, coef_in, top_x, top_z, low_x, low_z,
+    sent, came, s0, ready,
 ):
     f32 = jnp.float32
     cx, cy = flip.shape[0], flip.shape[1]
@@ -140,19 +140,26 @@
         corner1[1, y : y + 1, :] = vec[1, 0, y, 0:1, :]
     pl.semaphore_wait(barrier, len(greeted))
 
-    def send(src, dst, shift, sends, recvs, which):
-        copy = pltpu.make_async_remote_copy(
-            src_ref=src, dst_ref=dst, send_sem=sends.at[which], recv_sem=recvs.at[which],
+    def remote(src, dst, shift, out, into):
+        return pltpu.make_async_remote_copy(
+            src_ref=src, dst_ref=dst, send_sem=sent.at[out], recv_sem=came.at[into],
             device_id=device(shift), device_id_type=MESH,
         )
-        copy.start()
-        return copy
-
-    one = {
-        2: send(vec.at[1:3, 0], hx, (-1, 0, 0), s1, r1, 2),
-        5: send(corner1.at[1], hc.at[1], (-1, 0, -1), s1, r1, 5),
-        3: send(pack1, hz, (0, 0, -1), s1, r1, 3),
-    }
+
+    def send(src, dst, shift, out, into):
+        remote(src, dst, shift, out, into).start()
+
+    def arrived(ref, into):
+        remote(ref, ref, (0, 1, 0), 0, into).wait_recv()
+
+    def left(ref, out):
+        remote(ref, ref, (0, 1, 0), out, 0).wait_send()
+
+    send(vec.at[2, 0], hx.at[1], (-1, 0, 0), 0, 0)
+    send(pack1.at[0], hz.at[0], (0, 0, -1), 1, 1)
+    send(corner1.at[1], hc.at[0], (-1, 0, -1), 2, 2)
+    send(vec.at[1, 0], hx.at[0], (-1, 0, 0), 0, 3)
+    send(pack1.at[1], hz.at[1], (0, 0, -1), 1, 4)
     for shift in ((0, 1, 0), (1, 1, 0), (-1, 1, 0), (0, 1, 1), (0, 1, -1)):
         signal(ready, shift)
 
@@ -176,8 +183,12 @@
         mass[rows, :] = jnp.broadcast_to(flat[2, :, q : q + 1] * w, (ne, lanes))
 
     line_c, line_s = CLOSED[:, ORDER], COLLOC @ CLOSED[:, ORDER]
-    face_dofs = [(a * 4 + 3) * 4 + c for a in range(3) for c in range(4)]
-    face_dofs += [96 + (a * 4 + 3) * 3 + c for a in range(4) for c in range(3)]
+
+    def plane_dofs(b):
+        found = [(a * 4 + b) * 4 + c for a in range(3) for c in range(4)]
+        return found + [96 + (a * 4 + b) * 3 + c for a in range(4) for c in range(3)]
+
+    face_dofs = plane_dofs(ORDER)
 
     def quad_rows(ref, base, qx, qy):
         first = base + (qx * 16 + qy * 4) * ne
@@ -202,7 +213,7 @@
     for t, value in enumerate(summed):
         packed = jnp.where(lane == t, value, packed)
     coef[...] = packed
-    one[7] = send(coef, coef_in, (0, 1, 0), s1, r1, 7)
+    send(coef, coef_in, (0, 1, 0), 4, 7)
 
     def homes(comp, axis, low, high):
         found = []
@@ -230,10 +241,10 @@
         for offset, length, row, stride in places(comp, axis, at, low, high):
             elem[pl.ds(row, length, stride=stride), :] = load(offset, offset + length)
 
-    def face_places(comp, x, low, high):
+    def face_places(comp, x, low, high, layer=cy - 1):
         for fx in homes(comp, 0, x, x + 1):
             for fz in homes(comp, 2, low, high):
-                e = (fx[0] * cy + cy - 1) * cz + fz[0]
+                e = (fx[0] * cy + layer) * cz + fz[0]
                 d = comp // 2 * 12 + fx[1] * dims_of(comp)[2] + fz[1]
                 yield fz[2], fz[3], d * ne + e
 
@@ -253,32 +264,33 @@
     for comp in (0, 2):
         for x in range(size[0]):
             put_face(face_own, comp, x, 0, size[2], lambda a, b: vec[comp, x, 0, a:b, :])
-    top_x[...] = jnp.zeros_like(top_x)
-    top_z[...] = jnp.zeros_like(top_z)
     results = (res_x, res_y, res_z)
-    for res in results:
+    for res in (top_x, top_z, low_x, low_z) + results:
         res[...] = jnp.zeros_like(res)
 
     pl.semaphore_wait(ready, 5)
-    one[4] = send(corner1.at[0], hc.at[0], (0, -1, -1), s1, r1, 4)
-    one[6] = send(vec.at[2, 0, 0], hc.at[2], (-1, -1, 0), s1, r1, 6)
-    one[0] = send(vec.at[0, :, 0], hy.at[0], (0, -1, 0), s1, r1, 0)
-    one[1] = send(vec.at[2, :, 0], hy.at[1], (0, -1, 0), s1, r1, 1)
+    send(corner1.at[0], hc.at[1], (0, -1, -1), 2, 6)
+    send(vec.at[2, 0, 0], hc.at[2], (-1, -1, 0), 2, 6)
+    send(vec.at[0, :, 0], hy.at[0], (0, -1, 0), 3, 5)
+    send(vec.at[2, :, 0], hy.at[1], (0, -1, 0), 3, 5)
 
     def take_halo(comp):
         if comp == 1:
-            for which in (2, 5, 3):
-                one[which].wait_recv()
+            arrived(hc.at[0], 2)
+            arrived(hx.at[0], 3)
+            arrived(hz.at[1], 4)
             for y in range(size[1]):
                 put(1, 2, (size[0], y, 0), 0, size[2], lambda a, b: hx[0, y, a:b, :])
             for x in range(size[0]):
                 put(1, 1, (x, 0, size[2]), 0, size[1], lambda a, b: hz[1, x, a:b, :])
-            put(1, 1, (size[0], 0, size[2]), 0, size[1], lambda a, b: hc[1, a:b, :])
+            put(1, 1, (size[0], 0, size[2]), 0, size[1], lambda a, b: hc[0, a:b, :])
         elif comp == 0:
+            arrived(hz.at[0], 1)
             for x in range(size[0]):
                 put(0, 1, (x, 0, size[2]), 0, size[1], lambda a, b: hz[0, x, a:b, :])
                 put_face(face_own, 0, x, size[2], size[2] + 1, lambda a, b: hz[0, x, 0:1, :])
         else:
+            arrived(hx.at[1], 0)
             for y in range(size[1]):
                 put(2, 2, (size[0], y, 0), 0, size[2], lambda a, b: hx[1, y, a:b, :])
             put_face(face_own, 2, size[0], 0, size[2], lambda a, b: hx[1, 0, a:b, :])
@@ -316,7 +328,7 @@
     def mid_dims(comp):
         return [ORDER if axis == comp else QUAD for axis in range(3)]
 
-    for comp in (1, 0, 2):
+    def evaluate(comp):
         take_halo(comp)
         dims = dims_of(comp)
         base = comp * 48 * ne
@@ -340,7 +352,7 @@
 
     part = 64 * ne
 
-    for c in range(3):
+    def turn_of(c):
         p, r = [t for t in range(3) if t != c]
         flipped = -1 if c == 1 else 1
         for at in range(QUAD):
@@ -355,12 +367,18 @@
             scale = load_plane(curlw, 0, c, at, full)
             store_plane(cq, c * part, c, at, full, [k * w for k, w in zip(curl, scale)])
 
+    evaluate(2)
+    evaluate(0)
+    turn_of(1)
+    evaluate(1)
+    turn_of(0)
+    turn_of(2)
+
     closed_t, opened_t, colloc_t = CLOSED.T, OPENED.T, COLLOC.T
-    packs = (pack2_x, pack2_y, pack2_z)
+    packs = (pack2_x, pack2_y)
     near = (near_x, near_y, near_z)
     last = (last_x, last_y, last_z)
     orders = ((0, 1, 2), (0, 1, 2), (0, 2, 1))
-    sends = {0: [], 1: [], 2: []}
 
     def face_values(ref, signs):
         at = [ref[t * ne : (t + 1) * ne, :] * signs[t] for t in range(24)]
@@ -386,46 +404,60 @@
                 t = 12 + a * 3 + c
                 face_out[t * ne : (t + 1) * ne, :] = y * signs[t]
 
-    v_x, v_z, b = [], [], []
-    for qx in range(QUAD):
-        t_x, t_z, t_b = [], [], []
-        for qy in range(QUAD):
-            m = quad_rows(mass, 0, qx, qy) * np.float32(line_c[qy])
-            slope = np.float32(line_s[qy])
-            t_x += [m * quad_rows(uq, 0, qx, qy), -slope * quad_rows(cq, 2 * part, qx, qy)]
-            t_z += [m * quad_rows(uq, 2 * part, qx, qy), slope * quad_rows(cq, 0, qx, qy)]
-            t_b += [np.float32(line_c[qy]) * quad_rows(cq, part, qx, qy)]
-        v_x.append(add_all(t_x))
-        v_z.append(add_all(t_z))
-        b.append(add_all(t_b))
-    own_signs = [sign[d * ne : (d + 1) * ne, :] for d in face_dofs]
-    face_gradient(v_x, v_z, b, own_signs)
-    for comp, top in ((0, top_x), (2, top_z)):
-        for x in range(top.shape[0]):
-            for offset, length, row in face_places(comp, x, 0, top.shape[1]):
-                top[x, offset : offset + length, :] += face_out[pl.ds(row, length, stride=ne), :]
+    def plane_fields(values, slopes):
+        v_x, v_z, b = [], [], []
+        for qx in range(QUAD):
+            t_x, t_z, t_b = [], [], []
+            for qy in range(QUAD):
+                m = quad_rows(mass, 0, qx, qy) * np.float32(values[qy])
+                slope = np.float32(slopes[qy])
+                t_x += [m * quad_rows(uq, 0, qx, qy), -slope * quad_rows(cq, 2 * part, qx, qy)]
+                t_z += [m * quad_rows(uq, 2 * part, qx, qy), slope * quad_rows(cq, 0, qx, qy)]
+                t_b += [np.float32(values[qy]) * quad_rows(cq, part, qx, qy)]
+            v_x.append(add_all(t_x))
+            v_z.append(add_all(t_z))
+            b.append(add_all(t_b))
+        return v_x, v_z, b
+
+    def signs_of(dofs):
+        return [sign[d * ne : (d + 1) * ne, :] for d in dofs]
 
     def send_corner(comp, shift, slot, load):
         where = 4 * comp + slot
         for t in range(size[comp]):
             corner2[where, t : t + 1, :] = load(t)
-        sends[comp].append(
-            send(corner2.at[where], rc.at[where], shift, s2, r2, 8 * comp + slot)
-        )
-
-    for s in (0, 1):
-        send_corner(0, (0, 1, 2 * s - 1), 2 + s, lambda t: top_x[t, s * size[2] : s * size[2] + 1, :])
-        send_corner(2, (2 * s - 1, 1, 0), 2 * s + 1, lambda t: top_z[s * size[0], t : t + 1, :])
-    sends[0].append(send(top_x, near_x.at[1], (0, 1, 0), s2, r2, 5))
-    sends[2].append(send(top_z, last_z.at[1], (0, 1, 0), s2, r2, 16 + 7))
-
-    for which in (0, 1, 4, 6):
-        one[which].wait_recv()
+        send(corner2.at[where], rc.at[where], shift, 5 + comp, 8 + comp)
+
+    def send_plane(side, plane_x, plane_z):
+        b, layer = side * ORDER, side * (cy - 1)
+        fields = plane_fields(CLOSED[:, b], COLLOC @ CLOSED[:, b])
+        face_gradient(*fields, signs_of(plane_dofs(b)))
+        for comp, plane in ((0, plane_x), (2, plane_z)):
+            for x in range(plane.shape[0]):
+                for offset, length, row in face_places(comp, x, 0, plane.shape[1], layer):
+                    plane[x, offset : offset + length, :] += face_out[
+                        pl.ds(row, length, stride=ne), :
+                    ]
+        way = 2 * side - 1
+        for s in (0, 1):
+            z, x = s * size[2], s * size[0]
+            send_corner(0, (0, way, 2 * s - 1), 2 * side + s, lambda t: plane_x[t, z : z + 1, :])
+            send_corner(2, (2 * s - 1, way, 0), 2 * s + side, lambda t: plane_z[x, t : t + 1, :])
+        send(plane_x, near_x.at[side], (0, way, 0), 8, 11)
+        send(plane_z, last_z.at[side], (0, way, 0), 13, 16)
+
+    send_plane(1, top_x, top_z)
+    if cy > 1:
+        send_plane(0, low_x, low_z)
+
+    arrived(hy, 5)
+    arrived(hc.at[1:3], 6)
     for x in range(size[0]):
         put_face(face, 0, x, 0, size[2], lambda a, b: hy[0, x, a:b, :])
-        put_face(face, 0, x, size[2], size[2] + 1, lambda a, b: hc[0, x : x + 1, :])
+        put_face(face, 0, x, size[2], size[2] + 1, lambda a, b: hc[1, x : x + 1, :])
         put_face(face, 2, x, 0, size[2], lambda a, b: hy[1, x, a:b, :])
     put_face(face, 2, size[0], 0, size[2], lambda a, b: hc[2, a:b, :])
+    own_signs = signs_of(face_dofs)
     u_x, u_z, turn = face_values(face, own_signs)
     for qx in range(QUAD):
         for qy in range(QUAD):
@@ -439,9 +471,12 @@
             cq[part + first : part + first + 4 * ne, :] += (w * value) * turn[qx]
             cq[2 * part + first : 2 * part + first + 4 * ne, :] -= sloped * u_x[qx]
 
-    for comp in (1, 0, 2):
-        if comp == 0:
-            one[7].wait_recv()
+    if cy == 1:
+        send_plane(0, low_x, low_z)
+
+    for comp in (1, 2, 0):
+        if comp == 2:
+            arrived(coef_in, 7)
             theirs = [
                 jnp.broadcast_to(coef_in[:, t : t + 1], (ne, lanes)) for t in range(56)
             ]
@@ -487,67 +522,41 @@
                     res[first, middle, offset : offset + length, :] += elem[
                         pl.ds(row, length, stride=stride), :
                     ]
-        rim = order[1] if comp == 0 else order[0]
-        open_size, rim_size, last_size = size[comp], size[rim], size[order[2]]
-
-        def corner(s_rim, s_last):
-            shift = [0, 0, 0]
-            shift[rim], shift[order[2]] = 2 * s_rim - 1, 2 * s_last - 1
-            edge, row = s_rim * rim_size, s_last * last_size
-
-            def load(t):
-                f, m = (t, edge) if comp == 0 else (edge, t)
-                return res[f, m, row : row + 1, :]
-
-            send_corner(comp, shift, 2 * s_rim + s_last, load)
-
-        def send_near(src, side):
-            shift = [0, 0, 0]
-            shift[rim] = 2 * side - 1
-            sends[comp].append(send(src, near[comp].at[side], shift, s2, r2, 8 * comp + 4 + side))
-
-        def send_last(side):
-            shift = [0, 0, 0]
-            shift[order[2]] = 2 * side - 1
-            row = side * last_size
-            for f in range(res.shape[0]):
-                for m in range(res.shape[1]):
-                    packs[comp][side, f, m : m + 1, :] = res[f, m, row : row + 1, :]
-            sends[comp].append(
-                send(packs[comp].at[side], last[comp].at[side], shift, s2, r2, 8 * comp + 6 + side)
-            )
-
-        if comp == 1:
-            for s_rim in (0, 1):
-                for s_last in (0, 1):
-                    corner(s_rim, s_last)
-            for side in (0, 1):
-                send_near(res.at[side * rim_size], side)
-            for side in (0, 1):
-                send_last(side)
-        elif comp == 0:
-            for s_last in (0, 1):
-                corner(0, s_last)
-            for f in range(res.shape[0]):
-                low_x[f] = res[f, 0]
-            send_near(low_x, 0)
-            for x in range(res.shape[0]):
+        if comp == 0:
+            for x in range(size[0]):
                 for offset, length, row in face_places(0, x, 0, res.shape[2]):
                     res[x, 0, offset : offset + length, :] += face_out[
                         pl.ds(row, length, stride=ne), :
                     ]
-            for side in (0, 1):
-                send_last(side)
+        elif comp == 1:
+            for s_x in (0, 1):
+                for s_z in (0, 1):
+                    x, z = s_x * size[0], s_z * size[2]
+                    send_corner(
+                        1, (2 * s_x - 1, 0, 2 * s_z - 1), 2 * s_x + s_z,
+                        lambda t: res[x, t, z : z + 1, :],
+                    )
         else:
-            for s_rim in (0, 1):
-                corner(s_rim, 0)
-            send_last(0)
             for x in range(res.shape[0]):
                 for offset, length, row in face_places(2, x, 0, res.shape[1]):
                     for t in range(length):
                         res[x, offset + t, 0:1, :] += face_out[row + t * ne : row + t * ne + 1, :]
+        if comp > 0:
             for side in (0, 1):
-                send_near(res.at[side * rim_size], side)
+                send(
+                    res.at[side * size[0]], near[comp].at[side], (2 * side - 1, 0, 0),
+                    8 + comp, 11 + comp,
+                )
+        if comp < 2:
+            for side in (0, 1):
+                row = side * size[2]
+                for f in range(res.shape[0]):
+                    for m in range(res.shape[1]):
+                        packs[comp][side, f, m : m + 1, :] = res[f, m, row : row + 1, :]
+                send(
+                    packs[comp].at[side], last[comp].at[side], (0, 0, 2 * side - 1),
+                    11 + comp, 14 + comp,
+                )
 
     outs = (out_x, out_y, out_z)
     for comp in range(3):
@@ -555,8 +564,9 @@
     for comp in (1, 0, 2):
         out, order = outs[comp], orders[comp]
         rim = order[1] if comp == 0 else order[0]
-        for copy in sends[comp]:
-            copy.wait_recv()
+        arrived(rc.at[4 * comp : 4 * comp + 4], 8 + comp)
+        arrived(near[comp], 11 + comp)
+        arrived(last[comp], 14 + comp)
         for side in (0, 1):
             edge = (1 - side) * size[rim]
             row = (1 - side) * size[order[2]]
@@ -574,8 +584,12 @@
                 for t in range(size[comp]):
                     f, m = (t, edge) if comp == 0 else (edge, t)
                     out[f, m, row : row + 1, :] += rc[where, t : t + 1, :]
-    for copy in list(one.values()) + sends[0] + sends[1] + sends[2]:
-        copy.wait_send()
+    for out, ref in enumerate((hx, hz, hc, hy, coef)):
+        left(ref, out)
+    for comp in range(3):
+        left(rc.at[4 * comp : 4 * comp + 4], 5 + comp)
+        left(near[comp], 8 + comp)
+        left(last[comp], 11 + comp)
 
 
 def write_out(from_x, from_y, from_z, to_x, to_y, to_z, sems):
@@ -606,11 +620,11 @@
         *shapes,
         (2, sx, sy, lanes), (2, longest, lanes),
         (2, sy, sz, lanes), (2, sx, sz, lanes), (2, sx, sy, lanes), (3, longest, lanes),
-        *faces, (12, longest, lanes),
+        *faces[:2], (12, longest, lanes),
         (2, sx, sz + 1, lanes), (2, sy, sz + 1, lanes), (2, sz, sy + 1, lanes),
         *faces, (12, longest, lanes),
         (24 * ne, lanes), (24 * ne, lanes), (24 * ne, lanes), (ne, lanes), (ne, lanes),
-        (sx, sz + 1, lanes), (sx + 1, sz, lanes), (sx, sz + 1, lanes),
+        (sx, sz + 1, lanes), (sx + 1, sz, lanes), (sx, sz + 1, lanes), (sx + 1, sz, lanes),
     ]
     vmem = pl.BlockSpec(memory_space=pltpu.VMEM)
     padded = [s[0] * s[1] * (s[2] + -s[2] % 8) * lanes * 4 for s in shapes]
@@ -625,8 +639,7 @@
         out_specs=[vmem] * 3,
         scratch_shapes=[pltpu.VMEM(a.shape, a.dtype) for a in arguments]
         + [pltpu.VMEM(s, f32) for s in scratch]
-        + [pltpu.SemaphoreType.DMA((8,))] * 2
-        + [pltpu.SemaphoreType.DMA((24,))] * 2
+        + [pltpu.SemaphoreType.DMA((14,)), pltpu.SemaphoreType.DMA((17,))]
         + [pltpu.SemaphoreType.DMA((4,)), pltpu.SemaphoreType.REGULAR],
         compiler_params=pltpu.CompilerParams(
             collective_id=0, has_side_effects=True, vmem_limit_bytes=VMEM_ALL - room

time: 16.8 us -> 15.7 us (0.935)
  Pallas kernels: 16 us -> 14.9 us
    pallas_call x1, Pallas kernels: 15.2 us -> 14.1 us  [on_device(): pl.pallas_call(functools.partial(kernel, mesh_sizes), out_shape=[pltpu.VM...]
where the time goes in v2:
time: 15.7 us; the launch traced here: 15.5 us
  Pallas kernels  14.9 us (95%)
  between operations  0.64 us (4%)
    pallas_call x1, Pallas kernels, on_device(): pl.pallas_call(functools.partial(kernel, mesh_sizes), out_shape=[pltpu.VM...  14.1 us
    pallas_call x1, Pallas kernels, on_device(): pl.pallas_call(write_out, out_shape=outs, in_specs=[pl.BlockSpec(memory_s...  0.79 us

profile of v2, /device:TPU:0, one launch (start us, length us, event | category | flops | bytes accessed | tf_op | source)
XLA Modules:
  0.0 15.5 jit_solution(18402300237828950741)
XLA Ops:
  0.6 14.1 %curl_mass.1 = (f32[6,7,7,128]{3,2,1,0:T(8,128)S(1)}, f32[7,6,7,128]{3,2,1,0:T(8,128)S(1)}, f32[7,6,7,128]{3,2,1,0:T(8,128)S(1)}) custom-call(f32[3,6,6,6,128]{4,3,2,1,0:T(8,128)} %vec_hbm.1, s32[2,2,288]{2,1,0:T(2,128)} %flip_hbm.1, f32[2,2,128]{2,1,0:T(2,128)} %reluct_hbm.1, f32[2,2,128]{2,1,0:T(2,128)} %conduct_hbm.1), custom_call_target="tpu_custom_call" | custom-call | tf_op jit(solution)/shard_map/curl_mass/pallas_call | solution.py:635
  14.7 0.8 %write_out.1 = (f32[6,7,7,128]{3,2,1,0:T(8,128)}, f32[7,6,7,128]{3,2,1,0:T(8,128)}, f32[7,6,7,128]{3,2,1,0:T(8,128)}) custom-call(f32[6,7,7,128]{3,2,1,0:T(8,128)S(1)} %get-tuple-element.9.from_x, f32[7,6,7,128]{3,2,1,0:T(8,128)S(1)} %get-tuple-element.10.from_y, f32[7,6,7,128]{3,2,1,0:T(8,128)S(1)} %get-tuple-element.11.from_z), custom_call_target="tpu_custom_call" | custom-call | tf_op jit(solution)/shard_map/write_out/pallas_call | solution.py:649

commit v3 on v2

--- a/solution.py
+++ b/solution.py
@@ -352,27 +352,34 @@
 
     part = 64 * ne
 
-    def turn_of(c):
-        p, r = [t for t in range(3) if t != c]
-        flipped = -1 if c == 1 else 1
+    def half_turn(c, axis, at):
+        other = 3 - c - axis
+        u = load_plane(uq, other * part, c, at, full)
+        if axis < other:
+            return apply(COLLOC, u, -1)
+        return swap(apply(COLLOC, swap(u, ne), -1), ne)
+
+    def turn_of(c, axis, kept):
+        plus = (axis - c) % 3 == 1
         for at in range(QUAD):
-            u_p = load_plane(uq, p * part, c, at, full)
-            u_r = load_plane(uq, r * part, c, at, full)
-            along_p = apply(COLLOC, u_r, -1)
-            along_r = swap(apply(COLLOC, swap(u_p, ne), -1), ne)
-            if flipped > 0:
-                curl = [f - g for f, g in zip(along_p, along_r)]
+            one = half_turn(c, axis, at)
+            if kept:
+                two = load_plane(cq, c * part, c, at, full)
             else:
-                curl = [g - f for f, g in zip(along_p, along_r)]
+                two = half_turn(c, 3 - c - axis, at)
+            both = [a - b if plus else b - a for a, b in zip(one, two)]
             scale = load_plane(curlw, 0, c, at, full)
-            store_plane(cq, c * part, c, at, full, [k * w for k, w in zip(curl, scale)])
+            store_plane(cq, c * part, c, at, full, [k * w for k, w in zip(both, scale)])
 
     evaluate(2)
     evaluate(0)
-    turn_of(1)
+    turn_of(1, 2, False)
+    for c in (0, 2):
+        for at in range(QUAD):
+            store_plane(cq, c * part, c, at, full, half_turn(c, 1, at))
     evaluate(1)
-    turn_of(0)
-    turn_of(2)
+    turn_of(0, 2, True)
+    turn_of(2, 0, True)
 
     closed_t, opened_t, colloc_t = CLOSED.T, OPENED.T, COLLOC.T
     packs = (pack2_x, pack2_y)
@@ -422,13 +429,15 @@
     def signs_of(dofs):
         return [sign[d * ne : (d + 1) * ne, :] for d in dofs]
 
-    def send_corner(comp, shift, slot, load):
+    def pack_corner(comp, slot, load):
+        for t in range(size[comp]):
+            corner2[4 * comp + slot, t : t + 1, :] = load(t)
+
+    def send_corner(comp, shift, slot):
         where = 4 * comp + slot
-        for t in range(size[comp]):
-            corner2[where, t : t + 1, :] = load(t)
         send(corner2.at[where], rc.at[where], shift, 5 + comp, 8 + comp)
 
-    def send_plane(side, plane_x, plane_z):
+    def make_plane(side, plane_x, plane_z):
         b, layer = side * ORDER, side * (cy - 1)
         fields = plane_fields(CLOSED[:, b], COLLOC @ CLOSED[:, b])
         face_gradient(*fields, signs_of(plane_dofs(b)))
@@ -438,20 +447,33 @@
                     plane[x, offset : offset + length, :] += face_out[
                         pl.ds(row, length, stride=ne), :
                     ]
+        for s in (0, 1):
+            z, x = s * size[2], s * size[0]
+            pack_corner(0, 2 * side + s, lambda t: plane_x[t, z : z + 1, :])
+            pack_corner(2, 2 * s + side, lambda t: plane_z[x, t : t + 1, :])
+
+    def send_plane(side, plane_x, plane_z):
         way = 2 * side - 1
         for s in (0, 1):
-            z, x = s * size[2], s * size[0]
-            send_corner(0, (0, way, 2 * s - 1), 2 * side + s, lambda t: plane_x[t, z : z + 1, :])
-            send_corner(2, (2 * s - 1, way, 0), 2 * s + side, lambda t: plane_z[x, t : t + 1, :])
+            send_corner(0, (0, way, 2 * s - 1), 2 * side + s)
+            send_corner(2, (2 * s - 1, way, 0), 2 * s + side)
         send(plane_x, near_x.at[side], (0, way, 0), 8, 11)
         send(plane_z, last_z.at[side], (0, way, 0), 13, 16)
 
-    send_plane(1, top_x, top_z)
+    far = me[1] == mesh_sizes[1] - 1
+    make_plane(1, top_x, top_z)
+
+    @pl.when(far)
+    def _():
+        send_plane(1, top_x, top_z)
+
+    if cy > 1:
+        make_plane(0, low_x, low_z)
+
+    arrived(hy, 5)
+    arrived(hc.at[1:3], 6)
     if cy > 1:
         send_plane(0, low_x, low_z)
-
-    arrived(hy, 5)
-    arrived(hc.at[1:3], 6)
     for x in range(size[0]):
         put_face(face, 0, x, 0, size[2], lambda a, b: hy[0, x, a:b, :])
         put_face(face, 0, x, size[2], size[2] + 1, lambda a, b: hc[1, x : x + 1, :])
@@ -472,6 +494,7 @@
             cq[2 * part + first : 2 * part + first + 4 * ne, :] -= sloped * u_x[qx]
 
     if cy == 1:
+        make_plane(0, low_x, low_z)
         send_plane(0, low_x, low_z)
 
     for comp in (1, 2, 0):
@@ -532,10 +555,8 @@
             for s_x in (0, 1):
                 for s_z in (0, 1):
                     x, z = s_x * size[0], s_z * size[2]
-                    send_corner(
-                        1, (2 * s_x - 1, 0, 2 * s_z - 1), 2 * s_x + s_z,
-                        lambda t: res[x, t, z : z + 1, :],
-                    )
+                    pack_corner(1, 2 * s_x + s_z, lambda t: res[x, t, z : z + 1, :])
+                    send_corner(1, (2 * s_x - 1, 0, 2 * s_z - 1), 2 * s_x + s_z)
         else:
             for x in range(res.shape[0]):
                 for offset, length, row in face_places(2, x, 0, res.shape[1]):
@@ -557,6 +578,11 @@
                     packs[comp].at[side], last[comp].at[side], (0, 0, 2 * side - 1),
                     11 + comp, 14 + comp,
                 )
+        if comp == 1:
+
+            @pl.when(jnp.logical_not(far))
+            def _():
+                send_plane(1, top_x, top_z)
 
     outs = (out_x, out_y, out_z)
     for comp in range(3):

time: 15.7 us -> 15.8 us (level)
  no operation moved by 1% of the time
where the time goes in v3:
time: 15.8 us; the launch traced here: 15.7 us
  Pallas kernels  15 us (95%)
  between operations  0.64 us (4%)
    pallas_call x1, Pallas kernels, on_device(): pl.pallas_call(functools.partial(kernel, mesh_sizes), out_shape=[pltpu.VM...  14.2 us
    pallas_call x1, Pallas kernels, on_device(): pl.pallas_call(write_out, out_shape=outs, in_specs=[pl.BlockSpec(memory_s...  0.79 us

profile of v3, /device:TPU:0, one launch (start us, length us, event | category | flops | bytes accessed | tf_op | source)
XLA Modules:
  0.0 15.7 jit_solution(57296896173474202)
XLA Ops:
  0.6 14.2 %curl_mass.1 = (f32[6,7,7,128]{3,2,1,0:T(8,128)S(1)}, f32[7,6,7,128]{3,2,1,0:T(8,128)S(1)}, f32[7,6,7,128]{3,2,1,0:T(8,128)S(1)}) custom-call(f32[3,6,6,6,128]{4,3,2,1,0:T(8,128)} %vec_hbm.1, s32[2,2,288]{2,1,0:T(2,128)} %flip_hbm.1, f32[2,2,128]{2,1,0:T(2,128)} %reluct_hbm.1, f32[2,2,128]{2,1,0:T(2,128)} %conduct_hbm.1), custom_call_target="tpu_custom_call" | custom-call | tf_op jit(solution)/shard_map/curl_mass/pallas_call | solution.py:661
  14.9 0.8 %write_out.1 = (f32[6,7,7,128]{3,2,1,0:T(8,128)}, f32[7,6,7,128]{3,2,1,0:T(8,128)}, f32[7,6,7,128]{3,2,1,0:T(8,128)}) custom-call(f32[6,7,7,128]{3,2,1,0:T(8,128)S(1)} %get-tuple-element.9.from_x, f32[7,6,7,128]{3,2,1,0:T(8,128)S(1)} %get-tuple-element.10.from_y, f32[7,6,7,128]{3,2,1,0:T(8,128)S(1)} %get-tuple-element.11.from_z), custom_call_target="tpu_custom_call" | custom-call | tf_op jit(solution)/shard_map/write_out/pallas_call | solution.py:675

commit v4 on v3

--- a/solution.py
+++ b/solution.py
@@ -95,7 +95,7 @@
     res_x, res_y, res_z, pack1, corner1, hx, hy, hz, hc, pack2_x, pack2_y, corner2,
     near_x, near_y, near_z, last_x, last_y, last_z, rc,
     face, face_own, face_out, coef, coef_in, top_x, top_z, low_x, low_z,
-    sent, came, s0, ready,
+    edge_out, edge_in, sent, came, s0, ready,
 ):
     f32 = jnp.float32
     cx, cy = flip.shape[0], flip.shape[1]
@@ -123,11 +123,16 @@
     for fetch in fetches:
         fetch.start()
     barrier = pltpu.get_barrier_semaphore()
-    greeted = (
-        (0, -1, 0), (1, 0, 0), (0, 0, 1), (1, 0, 1), (1, -1, 0), (-1, -1, 0), (0, -1, 1), (0, -1, -1),
-    )
+    first, final = me[1] == 0, me[1] == mesh_sizes[1] - 1
+    above = ((0, 1, 0), (1, 1, 0), (-1, 1, 0), (0, 1, 1), (0, 1, -1))
+    greeted = ((1, 0, 0), (0, 0, 1), (1, 0, 1)) + tuple((s[0], -1, s[2]) for s in above)
     for shift in greeted:
         signal(barrier, shift)
+
+    @pl.when(jnp.logical_not(final))
+    def _():
+        for shift in above:
+            signal(barrier, shift)
 
     fetches[0].wait()
     for comp in (0, 1):
@@ -138,7 +143,7 @@
         corner1[0, x : x + 1, :] = vec[0, x, 0, 0:1, :]
     for y in range(size[1]):
         corner1[1, y : y + 1, :] = vec[1, 0, y, 0:1, :]
-    pl.semaphore_wait(barrier, len(greeted))
+    pl.semaphore_wait(barrier, len(greeted) + jnp.where(first, 0, len(above)))
 
     def remote(src, dst, shift, out, into):
         return pltpu.make_async_remote_copy(
@@ -149,19 +154,27 @@
     def send(src, dst, shift, out, into):
         remote(src, dst, shift, out, into).start()
 
-    def arrived(ref, into):
-        remote(ref, ref, (0, 1, 0), 0, into).wait_recv()
-
-    def left(ref, out):
-        remote(ref, ref, (0, 1, 0), out, 0).wait_send()
+    def arrived(rows, into):
+        remote(elem.at[0:rows], elem.at[0:rows], (0, 1, 0), 0, into).wait_recv()
 
     send(vec.at[2, 0], hx.at[1], (-1, 0, 0), 0, 0)
-    send(pack1.at[0], hz.at[0], (0, 0, -1), 1, 1)
-    send(corner1.at[1], hc.at[0], (-1, 0, -1), 2, 2)
-    send(vec.at[1, 0], hx.at[0], (-1, 0, 0), 0, 3)
-    send(pack1.at[1], hz.at[1], (0, 0, -1), 1, 4)
-    for shift in ((0, 1, 0), (1, 1, 0), (-1, 1, 0), (0, 1, 1), (0, 1, -1)):
-        signal(ready, shift)
+    send(pack1.at[0], hz.at[0], (0, 0, -1), 0, 1)
+    send(corner1.at[1], hc.at[0], (-1, 0, -1), 0, 2)
+    send(vec.at[1, 0], hx.at[0], (-1, 0, 0), 0, 2)
+    send(pack1.at[1], hz.at[1], (0, 0, -1), 0, 2)
+
+    @pl.when(final)
+    def _():
+        for shift in above:
+            signal(ready, shift)
+
+    def send_down():
+        send(corner1.at[0], hc.at[1], (0, -1, -1), 0, 3)
+        send(vec.at[2, 0, 0], hc.at[2], (-1, -1, 0), 0, 3)
+        send(vec.at[0, :, 0], hy.at[0], (0, -1, 0), 0, 3)
+        send(vec.at[2, :, 0], hy.at[1], (0, -1, 0), 0, 3)
+
+    pl.when(jnp.logical_not(first))(send_down)
 
     for fetch in fetches[1:]:
         fetch.wait()
@@ -213,7 +226,7 @@
     for t, value in enumerate(summed):
         packed = jnp.where(lane == t, value, packed)
     coef[...] = packed
-    send(coef, coef_in, (0, 1, 0), 4, 7)
+    send(coef, coef_in, (0, 1, 0), 0, 4)
 
     def homes(comp, axis, low, high):
         found = []
@@ -268,29 +281,26 @@
     for res in (top_x, top_z, low_x, low_z) + results:
         res[...] = jnp.zeros_like(res)
 
-    pl.semaphore_wait(ready, 5)
-    send(corner1.at[0], hc.at[1], (0, -1, -1), 2, 6)
-    send(vec.at[2, 0, 0], hc.at[2], (-1, -1, 0), 2, 6)
-    send(vec.at[0, :, 0], hy.at[0], (0, -1, 0), 3, 5)
-    send(vec.at[2, :, 0], hy.at[1], (0, -1, 0), 3, 5)
+    @pl.when(first)
+    def _():
+        pl.semaphore_wait(ready, len(above))
+        send_down()
 
     def take_halo(comp):
         if comp == 1:
-            arrived(hc.at[0], 2)
-            arrived(hx.at[0], 3)
-            arrived(hz.at[1], 4)
+            arrived(hc.shape[1] + size[1] * size[2] + size[0] * size[1], 2)
             for y in range(size[1]):
                 put(1, 2, (size[0], y, 0), 0, size[2], lambda a, b: hx[0, y, a:b, :])
             for x in range(size[0]):
                 put(1, 1, (x, 0, size[2]), 0, size[1], lambda a, b: hz[1, x, a:b, :])
             put(1, 1, (size[0], 0, size[2]), 0, size[1], lambda a, b: hc[0, a:b, :])
         elif comp == 0:
-            arrived(hz.at[0], 1)
+            arrived(size[0] * size[1], 1)
             for x in range(size[0]):
                 put(0, 1, (x, 0, size[2]), 0, size[1], lambda a, b: hz[0, x, a:b, :])
                 put_face(face_own, 0, x, size[2], size[2] + 1, lambda a, b: hz[0, x, 0:1, :])
         else:
-            arrived(hx.at[1], 0)
+            arrived(size[1] * size[2], 0)
             for y in range(size[1]):
                 put(2, 2, (size[0], y, 0), 0, size[2], lambda a, b: hx[1, y, a:b, :])
             put_face(face_own, 2, size[0], 0, size[2], lambda a, b: hx[1, 0, a:b, :])
@@ -435,7 +445,7 @@
 
     def send_corner(comp, shift, slot):
         where = 4 * comp + slot
-        send(corner2.at[where], rc.at[where], shift, 5 + comp, 8 + comp)
+        send(corner2.at[where], rc.at[where], shift, 0, 8)
 
     def make_plane(side, plane_x, plane_z):
         b, layer = side * ORDER, side * (cy - 1)
@@ -457,23 +467,18 @@
         for s in (0, 1):
             send_corner(0, (0, way, 2 * s - 1), 2 * side + s)
             send_corner(2, (2 * s - 1, way, 0), 2 * s + side)
-        send(plane_x, near_x.at[side], (0, way, 0), 8, 11)
-        send(plane_z, last_z.at[side], (0, way, 0), 13, 16)
-
-    far = me[1] == mesh_sizes[1] - 1
+        send(plane_x, near_x.at[side], (0, way, 0), 0, 5)
+        send(plane_z, last_z.at[side], (0, way, 0), 0, 7)
+
     make_plane(1, top_x, top_z)
 
-    @pl.when(far)
-    def _():
-        send_plane(1, top_x, top_z)
+    send_plane(1, top_x, top_z)
 
     if cy > 1:
         make_plane(0, low_x, low_z)
-
-    arrived(hy, 5)
-    arrived(hc.at[1:3], 6)
-    if cy > 1:
         send_plane(0, low_x, low_z)
+
+    arrived(2 * size[0] * size[2] + 2 * hc.shape[1], 3)
     for x in range(size[0]):
         put_face(face, 0, x, 0, size[2], lambda a, b: hy[0, x, a:b, :])
         put_face(face, 0, x, size[2], size[2] + 1, lambda a, b: hc[1, x : x + 1, :])
@@ -481,17 +486,16 @@
     put_face(face, 2, size[0], 0, size[2], lambda a, b: hc[2, a:b, :])
     own_signs = signs_of(face_dofs)
     u_x, u_z, turn = face_values(face, own_signs)
+
+    def add_rows(ref, which, qx, qy, more):
+        first = which * part + (qx * 16 + qy * 4) * ne
+        ref[first : first + 4 * ne, :] += more
+
     for qx in range(QUAD):
         for qy in range(QUAD):
-            first = (qx * 16 + qy * 4) * ne
-            value, slope = np.float32(line_c[qy]), np.float32(line_s[qy])
-            w = curlw[first : first + 4 * ne, :]
-            sloped = w * slope
-            uq[first : first + 4 * ne, :] += value * u_x[qx]
-            uq[2 * part + first : 2 * part + first + 4 * ne, :] += value * u_z[qx]
-            cq[first : first + 4 * ne, :] += sloped * u_z[qx]
-            cq[part + first : part + first + 4 * ne, :] += (w * value) * turn[qx]
-            cq[2 * part + first : 2 * part + first + 4 * ne, :] -= sloped * u_x[qx]
+            sloped = quad_rows(curlw, 0, qx, qy) * np.float32(line_s[qy])
+            add_rows(cq, 0, qx, qy, sloped * u_z[qx])
+            add_rows(cq, 2, qx, qy, -sloped * u_x[qx])
 
     if cy == 1:
         make_plane(0, low_x, low_z)
@@ -499,17 +503,12 @@
 
     for comp in (1, 2, 0):
         if comp == 2:
-            arrived(coef_in, 7)
-            theirs = [
-                jnp.broadcast_to(coef_in[:, t : t + 1], (ne, lanes)) for t in range(56)
-            ]
-            u_x, u_z, turn = face_values(face_own, theirs[32:])
-            m2 = [jnp.concatenate(theirs[4 * qx : 4 * qx + 4], 0) for qx in range(QUAD)]
-            k2 = [jnp.concatenate(theirs[16 + 4 * qx : 20 + 4 * qx], 0) for qx in range(QUAD)]
-            face_gradient(
-                [m * u for m, u in zip(m2, u_x)], [m * u for m, u in zip(m2, u_z)],
-                [k * u for k, u in zip(k2, turn)], theirs[32:],
-            )
+            for qx in range(QUAD):
+                for qy in range(QUAD):
+                    value = np.float32(line_c[qy])
+                    add_rows(uq, 0, qx, qy, value * u_x[qx])
+                    add_rows(uq, 2, qx, qy, value * u_z[qx])
+                    add_rows(cq, 1, qx, qy, (quad_rows(curlw, 0, qx, qy) * value) * turn[qx])
         dims = dims_of(comp)
         base = comp * 48 * ne
         p, r = [t for t in range(3) if t != comp]
@@ -545,28 +544,17 @@
                     res[first, middle, offset : offset + length, :] += elem[
                         pl.ds(row, length, stride=stride), :
                     ]
-        if comp == 0:
-            for x in range(size[0]):
-                for offset, length, row in face_places(0, x, 0, res.shape[2]):
-                    res[x, 0, offset : offset + length, :] += face_out[
-                        pl.ds(row, length, stride=ne), :
-                    ]
-        elif comp == 1:
+        if comp == 1:
             for s_x in (0, 1):
                 for s_z in (0, 1):
                     x, z = s_x * size[0], s_z * size[2]
                     pack_corner(1, 2 * s_x + s_z, lambda t: res[x, t, z : z + 1, :])
                     send_corner(1, (2 * s_x - 1, 0, 2 * s_z - 1), 2 * s_x + s_z)
-        else:
-            for x in range(res.shape[0]):
-                for offset, length, row in face_places(2, x, 0, res.shape[1]):
-                    for t in range(length):
-                        res[x, offset + t, 0:1, :] += face_out[row + t * ne : row + t * ne + 1, :]
         if comp > 0:
             for side in (0, 1):
                 send(
                     res.at[side * size[0]], near[comp].at[side], (2 * side - 1, 0, 0),
-                    8 + comp, 11 + comp,
+                    0, 5 + comp,
                 )
         if comp < 2:
             for side in (0, 1):
@@ -576,23 +564,44 @@
                         packs[comp][side, f, m : m + 1, :] = res[f, m, row : row + 1, :]
                 send(
                     packs[comp].at[side], last[comp].at[side], (0, 0, 2 * side - 1),
-                    11 + comp, 14 + comp,
+                    0, 5 + comp,
                 )
-        if comp == 1:
-
-            @pl.when(jnp.logical_not(far))
-            def _():
-                send_plane(1, top_x, top_z)
+    arrived(ne, 4)
+    theirs = [jnp.broadcast_to(coef_in[:, t : t + 1], (ne, lanes)) for t in range(56)]
+    u_x, u_z, turn = face_values(face_own, theirs[32:])
+    m2 = [jnp.concatenate(theirs[4 * qx : 4 * qx + 4], 0) for qx in range(QUAD)]
+    k2 = [jnp.concatenate(theirs[16 + 4 * qx : 20 + 4 * qx], 0) for qx in range(QUAD)]
+    face_gradient(
+        [m * u for m, u in zip(m2, u_x)], [m * u for m, u in zip(m2, u_z)],
+        [k * u for k, u in zip(k2, turn)], theirs[32:],
+    )
+    for s in (0, 1):
+        for x in range(size[0]):
+            for _, _, row in face_places(0, x, s * size[2], s * size[2] + 1):
+                edge_out[s, x : x + 1, :] = face_out[row : row + 1, :]
+        for offset, length, row in face_places(2, s * size[0], 0, size[2]):
+            edge_out[2 + s, offset : offset + length, :] = face_out[
+                pl.ds(row, length, stride=ne), :
+            ]
+        send(edge_out.at[s], edge_in.at[s], (0, 0, 2 * s - 1), 0, 8)
+        send(edge_out.at[2 + s], edge_in.at[2 + s], (2 * s - 1, 0, 0), 0, 8)
 
     outs = (out_x, out_y, out_z)
     for comp in range(3):
         outs[comp][...] = results[comp][...]
+    for x in range(size[0]):
+        for offset, length, row in face_places(0, x, 0, size[2] + 1):
+            out_x[x, 0, offset : offset + length, :] += face_out[pl.ds(row, length, stride=ne), :]
+    for x in range(size[0] + 1):
+        for offset, length, row in face_places(2, x, 0, size[2]):
+            for t in range(length):
+                out_z[x, offset + t, 0:1, :] += face_out[row + t * ne : row + t * ne + 1, :]
+    def rim_of(comp):
+        return orders[comp][1] if comp == 0 else orders[comp][0]
+
     for comp in (1, 0, 2):
-        out, order = outs[comp], orders[comp]
-        rim = order[1] if comp == 0 else order[0]
-        arrived(rc.at[4 * comp : 4 * comp + 4], 8 + comp)
-        arrived(near[comp], 11 + comp)
-        arrived(last[comp], 14 + comp)
+        out, order, rim = outs[comp], orders[comp], rim_of(comp)
+        arrived(2 * size[comp] * (size[rim] + size[order[2]] + 2), 5 + comp)
         for side in (0, 1):
             edge = (1 - side) * size[rim]
             row = (1 - side) * size[order[2]]
@@ -604,18 +613,26 @@
             for f in range(out.shape[0]):
                 for m in range(out.shape[1]):
                     out[f, m, row : row + 1, :] += last[comp][side, f, m : m + 1, :]
-            for s_last in (0, 1):
-                where = 4 * comp + 2 * side + s_last
-                row = (1 - s_last) * size[order[2]]
-                for t in range(size[comp]):
-                    f, m = (t, edge) if comp == 0 else (edge, t)
-                    out[f, m, row : row + 1, :] += rc[where, t : t + 1, :]
-    for out, ref in enumerate((hx, hz, hc, hy, coef)):
-        left(ref, out)
+    arrived((12 + 4) * rc.shape[1], 8)
     for comp in range(3):
-        left(rc.at[4 * comp : 4 * comp + 4], 5 + comp)
-        left(near[comp], 8 + comp)
-        left(last[comp], 11 + comp)
+        out, order, rim = outs[comp], orders[comp], rim_of(comp)
+        for slot in range(4):
+            edge = (1 - slot // 2) * size[rim]
+            row = (1 - slot % 2) * size[order[2]]
+            for t in range(size[comp]):
+                f, m = (t, edge) if comp == 0 else (edge, t)
+                out[f, m, row : row + 1, :] += rc[4 * comp + slot, t : t + 1, :]
+    for s in (0, 1):
+        z, x = (1 - s) * size[2], (1 - s) * size[0]
+        for t in range(size[0]):
+            out_x[t, 0, z : z + 1, :] += edge_in[s, t : t + 1, :]
+        for t in range(size[2]):
+            out_z[x, t, 0:1, :] += edge_in[2 + s, t : t + 1, :]
+    rows = ne + (3 + 12 + 4) * rc.shape[1]
+    for comp in range(3):
+        p, r = [size[t] for t in range(3) if t != comp]
+        rows += size[comp] * (p + r) + 2 * size[comp] * (p + r + 2)
+    remote(elem.at[0:rows], elem.at[0:rows], (0, 1, 0), 0, 0).wait_send()
 
 
 def write_out(from_x, from_y, from_z, to_x, to_y, to_z, sems):
@@ -651,6 +668,7 @@
         *faces, (12, longest, lanes),
         (24 * ne, lanes), (24 * ne, lanes), (24 * ne, lanes), (ne, lanes), (ne, lanes),
         (sx, sz + 1, lanes), (sx + 1, sz, lanes), (sx, sz + 1, lanes), (sx + 1, sz, lanes),
+        (4, longest, lanes), (4, longest, lanes),
     ]
     vmem = pl.BlockSpec(memory_space=pltpu.VMEM)
     padded = [s[0] * s[1] * (s[2] + -s[2] % 8) * lanes * 4 for s in shapes]
@@ -665,7 +683,7 @@
         out_specs=[vmem] * 3,
         scratch_shapes=[pltpu.VMEM(a.shape, a.dtype) for a in arguments]
         + [pltpu.VMEM(s, f32) for s in scratch]
-        + [pltpu.SemaphoreType.DMA((14,)), pltpu.SemaphoreType.DMA((17,))]
+        + [pltpu.SemaphoreType.DMA((1,)), pltpu.SemaphoreType.DMA((9,))]
         + [pltpu.SemaphoreType.DMA((4,)), pltpu.SemaphoreType.REGULAR],
         compiler_params=pltpu.CompilerParams(
             collective_id=0, has_side_effects=True, vmem_limit_bytes=VMEM_ALL - room

time: 15.8 us -> 15.4 us (0.975)
  Pallas kernels: 15 us -> 14.6 us
    pallas_call x1, Pallas kernels: 14.2 us -> 13.8 us  [on_device(): pl.pallas_call(functools.partial(kernel, mesh_sizes), out_shape=[pltpu.VM...]
where the time goes in v4:
time: 15.4 us; the launch traced here: 15.2 us
  Pallas kernels  14.6 us (95%)
  between operations  0.64 us (4%)
    pallas_call x1, Pallas kernels, on_device(): pl.pallas_call(functools.partial(kernel, mesh_sizes), out_shape=[pltpu.VM...  13.8 us
    pallas_call x1, Pallas kernels, on_device(): pl.pallas_call(write_out, out_shape=outs, in_specs=[pl.BlockSpec(memory_s...  0.79 us

profile of v4, /device:TPU:0, one launch (start us, length us, event | category | flops | bytes accessed | tf_op | source)
XLA Modules:
  0.0 15.2 jit_solution(9521751278376515055)
XLA Ops:
  0.6 13.8 %curl_mass.1 = (f32[6,7,7,128]{3,2,1,0:T(8,128)S(1)}, f32[7,6,7,128]{3,2,1,0:T(8,128)S(1)}, f32[7,6,7,128]{3,2,1,0:T(8,128)S(1)}) custom-call(f32[3,6,6,6,128]{4,3,2,1,0:T(8,128)} %vec_hbm.1, s32[2,2,288]{2,1,0:T(2,128)} %flip_hbm.1, f32[2,2,128]{2,1,0:T(2,128)} %reluct_hbm.1, f32[2,2,128]{2,1,0:T(2,128)} %conduct_hbm.1), custom_call_target="tpu_custom_call" | custom-call | tf_op jit(solution)/shard_map/curl_mass/pallas_call | solution.py:679
  14.4 0.8 %write_out.1 = (f32[6,7,7,128]{3,2,1,0:T(8,128)}, f32[7,6,7,128]{3,2,1,0:T(8,128)}, f32[7,6,7,128]{3,2,1,0:T(8,128)}) custom-call(f32[6,7,7,128]{3,2,1,0:T(8,128)S(1)} %get-tuple-element.9.from_x, f32[7,6,7,128]{3,2,1,0:T(8,128)S(1)} %get-tuple-element.10.from_y, f32[7,6,7,128]{3,2,1,0:T(8,128)S(1)} %get-tuple-element.11.from_z), custom_call_target="tpu_custom_call" | custom-call | tf_op jit(solution)/shard_map/write_out/pallas_call | solution.py:693

commit v5 on v4

--- a/solution.py
+++ b/solution.py
@@ -95,7 +95,7 @@
     res_x, res_y, res_z, pack1, corner1, hx, hy, hz, hc, pack2_x, pack2_y, corner2,
     near_x, near_y, near_z, last_x, last_y, last_z, rc,
     face, face_own, face_out, coef, coef_in, top_x, top_z, low_x, low_z,
-    edge_out, edge_in, sent, came, s0, ready,
+    edge_out, edge_in, low_out, sent, came, s0, ready,
 ):
     f32 = jnp.float32
     cx, cy = flip.shape[0], flip.shape[1]
@@ -123,13 +123,13 @@
     for fetch in fetches:
         fetch.start()
     barrier = pltpu.get_barrier_semaphore()
-    first, final = me[1] == 0, me[1] == mesh_sizes[1] - 1
+    lowest, highest = me[1] == 0, me[1] == mesh_sizes[1] - 1
     above = ((0, 1, 0), (1, 1, 0), (-1, 1, 0), (0, 1, 1), (0, 1, -1))
     greeted = ((1, 0, 0), (0, 0, 1), (1, 0, 1)) + tuple((s[0], -1, s[2]) for s in above)
     for shift in greeted:
         signal(barrier, shift)
 
-    @pl.when(jnp.logical_not(final))
+    @pl.when(jnp.logical_not(highest))
     def _():
         for shift in above:
             signal(barrier, shift)
@@ -143,7 +143,7 @@
         corner1[0, x : x + 1, :] = vec[0, x, 0, 0:1, :]
     for y in range(size[1]):
         corner1[1, y : y + 1, :] = vec[1, 0, y, 0:1, :]
-    pl.semaphore_wait(barrier, len(greeted) + jnp.where(first, 0, len(above)))
+    pl.semaphore_wait(barrier, len(greeted) + jnp.where(lowest, 0, len(above)))
 
     def remote(src, dst, shift, out, into):
         return pltpu.make_async_remote_copy(
@@ -163,7 +163,7 @@
     send(vec.at[1, 0], hx.at[0], (-1, 0, 0), 0, 2)
     send(pack1.at[1], hz.at[1], (0, 0, -1), 0, 2)
 
-    @pl.when(final)
+    @pl.when(highest)
     def _():
         for shift in above:
             signal(ready, shift)
@@ -174,7 +174,7 @@
         send(vec.at[0, :, 0], hy.at[0], (0, -1, 0), 0, 3)
         send(vec.at[2, :, 0], hy.at[1], (0, -1, 0), 0, 3)
 
-    pl.when(jnp.logical_not(first))(send_down)
+    pl.when(jnp.logical_not(lowest))(send_down)
 
     for fetch in fetches[1:]:
         fetch.wait()
@@ -281,10 +281,6 @@
     for res in (top_x, top_z, low_x, low_z) + results:
         res[...] = jnp.zeros_like(res)
 
-    @pl.when(first)
-    def _():
-        pl.semaphore_wait(ready, len(above))
-        send_down()
 
     def take_halo(comp):
         if comp == 1:
@@ -387,6 +383,11 @@
     for c in (0, 2):
         for at in range(QUAD):
             store_plane(cq, c * part, c, at, full, half_turn(c, 1, at))
+    @pl.when(lowest)
+    def _():
+        pl.semaphore_wait(ready, len(above))
+        send_down()
+
     evaluate(1)
     turn_of(0, 2, True)
     turn_of(2, 0, True)
@@ -407,7 +408,8 @@
         along_x = apply(COLLOC, u_z, -1)
         return u_x, u_z, [f - g for f, g in zip(along_z, along_x)]
 
-    def face_gradient(v_x, v_z, b, signs):
+    def face_gradient(v_x, v_z, b, signs, into=None):
+        into = face_out if into is None else into
         by_z = swap(apply(colloc_t, swap(b, ne), -1), ne)
         by_x = apply(colloc_t, b, -1)
         v_x = [v + f for v, f in zip(v_x, by_z)]
@@ -415,11 +417,11 @@
         for c, block in enumerate(apply(closed_t, swap(apply(opened_t, v_x), ne))):
             for a, y in enumerate(pieces_of(block)):
                 t = a * 4 + c
-                face_out[t * ne : (t + 1) * ne, :] = y * signs[t]
+                into[t * ne : (t + 1) * ne, :] = y * signs[t]
         for c, block in enumerate(apply(opened_t, swap(apply(closed_t, v_z), ne))):
             for a, y in enumerate(pieces_of(block)):
                 t = 12 + a * 3 + c
-                face_out[t * ne : (t + 1) * ne, :] = y * signs[t]
+                into[t * ne : (t + 1) * ne, :] = y * signs[t]
 
     def plane_fields(values, slopes):
         v_x, v_z, b = [], [], []
@@ -478,6 +480,28 @@
         make_plane(0, low_x, low_z)
         send_plane(0, low_x, low_z)
 
+    def low_lines():
+        arrived(ne, 4)
+        theirs = [jnp.broadcast_to(coef_in[:, t : t + 1], (ne, lanes)) for t in range(56)]
+        u_x, u_z, turn = face_values(face_own, theirs[32:])
+        m2 = [jnp.concatenate(theirs[4 * qx : 4 * qx + 4], 0) for qx in range(QUAD)]
+        k2 = [jnp.concatenate(theirs[16 + 4 * qx : 20 + 4 * qx], 0) for qx in range(QUAD)]
+        face_gradient(
+            [m * u for m, u in zip(m2, u_x)], [m * u for m, u in zip(m2, u_z)],
+            [k * u for k, u in zip(k2, turn)], theirs[32:], low_out,
+        )
+        for s in (0, 1):
+            for x in range(size[0]):
+                for _, _, row in face_places(0, x, s * size[2], s * size[2] + 1):
+                    edge_out[s, x : x + 1, :] = low_out[row : row + 1, :]
+            for offset, length, row in face_places(2, s * size[0], 0, size[2]):
+                edge_out[2 + s, offset : offset + length, :] = low_out[
+                    pl.ds(row, length, stride=ne), :
+                ]
+            send(edge_out.at[s], edge_in.at[s], (0, 0, 2 * s - 1), 0, 8)
+            send(edge_out.at[2 + s], edge_in.at[2 + s], (2 * s - 1, 0, 0), 0, 8)
+
+    pl.when(jnp.logical_not(lowest))(low_lines)
     arrived(2 * size[0] * size[2] + 2 * hc.shape[1], 3)
     for x in range(size[0]):
         put_face(face, 0, x, 0, size[2], lambda a, b: hy[0, x, a:b, :])
@@ -566,36 +590,18 @@
                     packs[comp].at[side], last[comp].at[side], (0, 0, 2 * side - 1),
                     0, 5 + comp,
                 )
-    arrived(ne, 4)
-    theirs = [jnp.broadcast_to(coef_in[:, t : t + 1], (ne, lanes)) for t in range(56)]
-    u_x, u_z, turn = face_values(face_own, theirs[32:])
-    m2 = [jnp.concatenate(theirs[4 * qx : 4 * qx + 4], 0) for qx in range(QUAD)]
-    k2 = [jnp.concatenate(theirs[16 + 4 * qx : 20 + 4 * qx], 0) for qx in range(QUAD)]
-    face_gradient(
-        [m * u for m, u in zip(m2, u_x)], [m * u for m, u in zip(m2, u_z)],
-        [k * u for k, u in zip(k2, turn)], theirs[32:],
-    )
-    for s in (0, 1):
-        for x in range(size[0]):
-            for _, _, row in face_places(0, x, s * size[2], s * size[2] + 1):
-                edge_out[s, x : x + 1, :] = face_out[row : row + 1, :]
-        for offset, length, row in face_places(2, s * size[0], 0, size[2]):
-            edge_out[2 + s, offset : offset + length, :] = face_out[
-                pl.ds(row, length, stride=ne), :
-            ]
-        send(edge_out.at[s], edge_in.at[s], (0, 0, 2 * s - 1), 0, 8)
-        send(edge_out.at[2 + s], edge_in.at[2 + s], (2 * s - 1, 0, 0), 0, 8)
+    pl.when(lowest)(low_lines)
 
     outs = (out_x, out_y, out_z)
     for comp in range(3):
         outs[comp][...] = results[comp][...]
     for x in range(size[0]):
         for offset, length, row in face_places(0, x, 0, size[2] + 1):
-            out_x[x, 0, offset : offset + length, :] += face_out[pl.ds(row, length, stride=ne), :]
+            out_x[x, 0, offset : offset + length, :] += low_out[pl.ds(row, length, stride=ne), :]
     for x in range(size[0] + 1):
         for offset, length, row in face_places(2, x, 0, size[2]):
             for t in range(length):
-                out_z[x, offset + t, 0:1, :] += face_out[row + t * ne : row + t * ne + 1, :]
+                out_z[x, offset + t, 0:1, :] += low_out[row + t * ne : row + t * ne + 1, :]
     def rim_of(comp):
         return orders[comp][1] if comp == 0 else orders[comp][0]
 
@@ -668,7 +674,7 @@
         *faces, (12, longest, lanes),
         (24 * ne, lanes), (24 * ne, lanes), (24 * ne, lanes), (ne, lanes), (ne, lanes),
         (sx, sz + 1, lanes), (sx + 1, sz, lanes), (sx, sz + 1, lanes), (sx + 1, sz, lanes),
-        (4, longest, lanes), (4, longest, lanes),
+        (4, longest, lanes), (4, longest, lanes), (24 * ne, lanes),
     ]
     vmem = pl.BlockSpec(memory_space=pltpu.VMEM)
     padded = [s[0] * s[1] * (s[2] + -s[2] % 8) * lanes * 4 for s in shapes]

time: 15.4 us -> 15.1 us (0.981)
  Pallas kernels: 14.6 us -> 14.3 us
    pallas_call x1, Pallas kernels: 13.8 us -> 13.5 us  [on_device(): pl.pallas_call(functools.partial(kernel, mesh_sizes), out_shape=[pltpu.VM...]
where the time goes in v5:
time: 15.1 us; the launch traced here: 14.9 us
  Pallas kernels  14.3 us (95%)
  between operations  0.64 us (4%)
    pallas_call x1, Pallas kernels, on_device(): pl.pallas_call(functools.partial(kernel, mesh_sizes), out_shape=[pltpu.VM...  13.5 us
    pallas_call x1, Pallas kernels, on_device(): pl.pallas_call(write_out, out_shape=outs, in_specs=[pl.BlockSpec(memory_s...  0.79 us

profile of v5, /device:TPU:0, one launch (start us, length us, event | category | flops | bytes accessed | tf_op | source)
XLA Modules:
  0.0 14.9 jit_solution(12063909604655804545)
XLA Ops:
  0.6 13.5 %curl_mass.1 = (f32[6,7,7,128]{3,2,1,0:T(8,128)S(1)}, f32[7,6,7,128]{3,2,1,0:T(8,128)S(1)}, f32[7,6,7,128]{3,2,1,0:T(8,128)S(1)}) custom-call(f32[3,6,6,6,128]{4,3,2,1,0:T(8,128)} %vec_hbm.1, s32[2,2,288]{2,1,0:T(2,128)} %flip_hbm.1, f32[2,2,128]{2,1,0:T(2,128)} %reluct_hbm.1, f32[2,2,128]{2,1,0:T(2,128)} %conduct_hbm.1), custom_call_target="tpu_custom_call" | custom-call | tf_op jit(solution)/shard_map/curl_mass/pallas_call | solution.py:685
  14.1 0.8 %write_out.1 = (f32[6,7,7,128]{3,2,1,0:T(8,128)}, f32[7,6,7,128]{3,2,1,0:T(8,128)}, f32[7,6,7,128]{3,2,1,0:T(8,128)}) custom-call(f32[6,7,7,128]{3,2,1,0:T(8,128)S(1)} %get-tuple-element.9.from_x, f32[7,6,7,128]{3,2,1,0:T(8,128)S(1)} %get-tuple-element.10.from_y, f32[7,6,7,128]{3,2,1,0:T(8,128)S(1)} %get-tuple-element.11.from_z), custom_call_target="tpu_custom_call" | custom-call | tf_op jit(solution)/shard_map/write_out/pallas_call | solution.py:699

commit v6 on v5

--- a/solution.py
+++ b/solution.py
@@ -380,13 +380,14 @@
     evaluate(2)
     evaluate(0)
     turn_of(1, 2, False)
-    for c in (0, 2):
-        for at in range(QUAD):
-            store_plane(cq, c * part, c, at, full, half_turn(c, 1, at))
     @pl.when(lowest)
     def _():
         pl.semaphore_wait(ready, len(above))
         send_down()
+
+    for c in (0, 2):
+        for at in range(QUAD):
+            store_plane(cq, c * part, c, at, full, half_turn(c, 1, at))
 
     evaluate(1)
     turn_of(0, 2, True)

time: 15.1 us -> 15.1 us (level)
  no operation moved by 1% of the time
where the time goes in v6:
time: 15.1 us; the launch traced here: 14.9 us
  Pallas kernels  14.3 us (95%)
  between operations  0.64 us (4%)
    pallas_call x1, Pallas kernels, on_device(): pl.pallas_call(functools.partial(kernel, mesh_sizes), out_shape=[pltpu.VM...  13.5 us
    pallas_call x1, Pallas kernels, on_device(): pl.pallas_call(write_out, out_shape=outs, in_specs=[pl.BlockSpec(memory_s...  0.79 us

profile of v6, /device:TPU:0, one launch (start us, length us, event | category | flops | bytes accessed | tf_op | source)
XLA Modules:
  0.0 14.9 jit_solution(10336040122465908442)
XLA Ops:
  0.6 13.5 %curl_mass.1 = (f32[6,7,7,128]{3,2,1,0:T(8,128)S(1)}, f32[7,6,7,128]{3,2,1,0:T(8,128)S(1)}, f32[7,6,7,128]{3,2,1,0:T(8,128)S(1)}) custom-call(f32[3,6,6,6,128]{4,3,2,1,0:T(8,128)} %vec_hbm.1, s32[2,2,288]{2,1,0:T(2,128)} %flip_hbm.1, f32[2,2,128]{2,1,0:T(2,128)} %reluct_hbm.1, f32[2,2,128]{2,1,0:T(2,128)} %conduct_hbm.1), custom_call_target="tpu_custom_call" | custom-call | tf_op jit(solution)/shard_map/curl_mass/pallas_call | solution.py:686
  14.1 0.8 %write_out.1 = (f32[6,7,7,128]{3,2,1,0:T(8,128)}, f32[7,6,7,128]{3,2,1,0:T(8,128)}, f32[7,6,7,128]{3,2,1,0:T(8,128)}) custom-call(f32[6,7,7,128]{3,2,1,0:T(8,128)S(1)} %get-tuple-element.9.from_x, f32[7,6,7,128]{3,2,1,0:T(8,128)S(1)} %get-tuple-element.10.from_y, f32[7,6,7,128]{3,2,1,0:T(8,128)S(1)} %get-tuple-element.11.from_z), custom_call_target="tpu_custom_call" | custom-call | tf_op jit(solution)/shard_map/write_out/pallas_call | solution.py:700
